TPU v7x, 8 devices: a whole 2x2x1 slice. The times are simulated.
8 devices in a mesh: local: 2 (over z, y), data: 4 (over x, core).
Axes of the slice: x: 2, y: 2, z: 1, core: 2. Of those that a mesh axis runs over, the one named last changes fastest.
Arguments:
- tokens: bfloat16 [16384, 1536], P(('local', 'data'))
- grad_out: bfloat16 [16384, 1536], P(('local', 'data'))
- w_up: bfloat16 [2, 1536, 8960], P(None, ('local', 'data'))
- w_down: bfloat16 [2, 8960, 1536], P(None, ('local', 'data'))
Outputs:
- output 1: bfloat16 [16384, 1536], P(('local', 'data'))
- output 2: bfloat16 [16384, 1536], P(('local', 'data'))
- output 3: float32 [2, 1536, 8960], P(None, ('local', 'data'))
- output 4: float32 [2, 8960, 1536], P(None, ('local', 'data'))
All inputs are finite; a program needn't handle non-finite values.
Results may differ from a plain program's by a relative error of at most 0.0119238.
Values are sent between devices in bfloat16 or wider.
A program may use at most 1 GiB of HBM per device.

v0:
```python
import jax
import jax.numpy as jnp
from jax import lax
from jax.sharding import PartitionSpec as P

NORM_EPS = 1e-6
BOTH_AXES = ('local', 'data')
CONTRACT_ROWS = (((0,), (0,)), ((), ()))
CONTRACT_COLS = (((1,), (1,)), ((), ()))


def rms_norm(x_f32):
    return x_f32 * lax.rsqrt(jnp.mean(x_f32 * x_f32, axis=-1, keepdims=True) + NORM_EPS)


def gelu_tanh(values):
    return jax.nn.gelu(values, approximate=True)


def solution(mesh):
    n_local = mesh.shape['local']
    tok_spec = P(BOTH_AXES, None)
    w_spec = P(None, BOTH_AXES, None)

    def device_fn(tokens, grad_out, w_up, w_down):
        num_layers = w_up.shape[0]
        loc_index = lax.axis_index('local')
        saved_acts = []
        hidden_state = tokens
        for layer_idx in range(num_layers):
            up_full = lax.all_gather(w_up[layer_idx], BOTH_AXES, axis=0, tiled=True)
            down_full = lax.all_gather(w_down[layer_idx], BOTH_AXES, axis=0, tiled=True)
            up_rows = up_full.shape[0] // n_local
            down_rows = down_full.shape[0] // n_local
            up_second = lax.dynamic_slice_in_dim(up_full, loc_index * up_rows, up_rows, axis=0)
            down_second = lax.dynamic_slice_in_dim(down_full, loc_index * down_rows, down_rows, axis=0)
            x_f32 = hidden_state.astype(jnp.float32)
            normed = rms_norm(x_f32).astype(jnp.bfloat16)
            pre_act = jnp.dot(normed, up_full, preferred_element_type=jnp.float32).astype(jnp.bfloat16)
            hidden = gelu_tanh(pre_act.astype(jnp.float32)).astype(jnp.bfloat16)
            saved_acts.append((hidden_state, normed, pre_act, hidden, up_second, down_second))
            hidden_state = (x_f32 + jnp.dot(hidden, down_full, preferred_element_type=jnp.float32)).astype(jnp.bfloat16)
        cotangent = grad_out
        grads_up = [None] * num_layers
        grads_down = [None] * num_layers
        for layer_idx in reversed(range(num_layers)):
            layer_in, normed, pre_act, hidden, up_second, down_second = saved_acts[layer_idx]
            up_full = lax.all_gather(up_second, 'local', axis=0, tiled=True)
            down_full = lax.all_gather(down_second, 'local', axis=0, tiled=True)
            down_part = lax.dot_general(hidden, cotangent, CONTRACT_ROWS, preferred_element_type=jnp.float32)
            d_hidden = lax.dot_general(cotangent, down_full, CONTRACT_COLS, preferred_element_type=jnp.float32).astype(jnp.bfloat16)
            _, gelu_back = jax.vjp(gelu_tanh, pre_act.astype(jnp.float32))
            d_pre = gelu_back(d_hidden.astype(jnp.float32))[0].astype(jnp.bfloat16)
            up_part = lax.dot_general(normed, d_pre, CONTRACT_ROWS, preferred_element_type=jnp.float32)
            d_normed = lax.dot_general(d_pre, up_full, CONTRACT_COLS, preferred_element_type=jnp.float32)
            _, norm_back = jax.vjp(rms_norm, layer_in.astype(jnp.float32))
            cotangent = (cotangent.astype(jnp.float32) + norm_back(d_normed)[0]).astype(jnp.bfloat16)
            grads_up[layer_idx] = lax.psum_scatter(up_part, BOTH_AXES, scatter_dimension=0, tiled=True)
            grads_down[layer_idx] = lax.psum_scatter(down_part, BOTH_AXES, scatter_dimension=0, tiled=True)
        return hidden_state, cotangent, jnp.stack(grads_up), jnp.stack(grads_down)

    return jax.shard_map(device_fn, mesh=mesh, in_specs=(tok_spec, tok_spec, w_spec, w_spec), out_specs=(tok_spec, tok_spec, w_spec, w_spec), check_vma=False)
```

profile of v0, /device:TPU:0, one launch (start us, length us, event | category | flops | bytes accessed | tf_op | source)
XLA Modules:
  0.0 3080.6 jit_solution(16543212264905886574)
XLA Ops:
  7.2 0.0 all-gather.23.cloned.1.call-start
  7.2 6.4 fusion.65
  13.6 0.0 all-gather.23.cloned.1.call-update
  13.6 0.0 all-gather.21.cloned.1.call-start
  13.6 6.4 fusion.64
  20.0 0.0 all-gather.21.cloned.1.call-update
  20.0 0.0 all-gather.19.cloned.1.call-start
  20.1 0.7 all-gather.19.cloned.1.call-update
  20.8 0.0 all-gather.17.cloned.1.call-start
  20.8 0.5 all-gather.17.cloned.1.call-update
  21.3 0.0 all-gather.25.cloned.1.call-start
  21.4 124.8 %all-gather.23.cloned.1.call-done = bf16[1,8960,1536]{2,1,0:T(8,128)(2,1)} async-done(((bf16[1,1120,1536]{2,1,0:T(8,128)(2,1)}), bf16[1,8960,1536]{2,1,0:T(8,128)(2,1)}) %all-gather.23.cloned.1.call-update) | async-done | bytes 27525136 | tf_op jit(solution)/shard_map/all_gather | solution.py:32
  146.2 12.9 constant_dynamic-slice_fusion.3
  159.1 0.0 all-gather.25.cloned.1.call-update
  159.1 0.0 all-gather.27.cloned.1.call-start
  159.2 119.0 %all-gather.21.cloned.1.call-done = bf16[1,1536,8960]{2,1,0:T(8,128)(2,1)} async-done(((bf16[1,192,8960]{2,1,0:T(8,128)(2,1)}), bf16[1,1536,8960]{2,1,0:T(8,128)(2,1)}) %all-gather.21.cloned.1.call-update) | async-done | bytes 27525136 | tf_op jit(solution)/shard_map/all_gather | solution.py:31
  278.2 13.0 constant_dynamic-slice_fusion.2
  291.1 0.0 all-gather.27.cloned.1.call-update
  291.2 0.0 all-gather.29.cloned.1.call-start
  291.2 119.0 %all-gather.19.cloned.1.call-done = bf16[1,8960,1536]{2,1,0:T(8,128)(2,1)} async-done(((bf16[1,1120,1536]{2,1,0:T(8,128)(2,1)}), bf16[1,8960,1536]{2,1,0:T(8,128)(2,1)}) %all-gather.19.cloned.1.call-update) | async-done | bytes 27525136 | tf_op jit(solution)/shard_map/all_gather | solution.py:32
  410.2 13.0 constant_dynamic-slice_fusion.1
  423.2 0.0 all-gather.29.cloned.1.call-update
  423.3 0.0 all-gather.31.cloned.1.call-start
  423.3 8.6 copy.8
  432.0 4.1 fusion.38
  436.1 0.6 copy-done.1
  436.7 104.9 %all-gather.17.cloned.1.call-done = bf16[1,1536,8960]{2,1,0:T(8,128)(2,1)} async-done(((bf16[1,192,8960]{2,1,0:T(8,128)(2,1)}), bf16[1,1536,8960]{2,1,0:T(8,128)(2,1)}) %all-gather.17.cloned.1.call-update) | async-done | bytes 27525136 | tf_op jit(solution)/shard_map/all_gather | solution.py:31
  541.5 66.4 %convolution_convert_fusion.1 = bf16[2048,8960]{1,0:T(8,128)(2,1)} fusion(bf16[1,1536,8960]{2,1,0:T(8,128)(2,1)} %all-gather.17.cloned.1.call-done, bf16[2048,1536]{0,1:T(8,128)(2,1)} %copy.8, f32[2048]{0:T(1024)S(1)} %fusion.56), kind=kOutput, calls=%fused_computation.35 | convolution fusion | flops 56399233024 | bytes 70524928 | tf_op jit(solution)/shard_map/dot_general | solution.py:39
  608.0 0.0 copy-done.3
  608.0 69.8 %fusion.42 = (f32[2048]{0:T(1024)S(1)}, bf16[2048,1536]{0,1:T(8,128)(2,1)}) fusion(bf16[1,8960,1536]{2,1,0:T(8,128)(2,1)} %all-gather.19.cloned.1.call-done, bf16[2048,8960]{1,0:T(8,128)(2,1)} %convolution_convert_fusion.1, bf16[2048,1536]{0,1:T(8,128)(2,1)} %copy.8), kind=kOutput, calls=%fused_computation.70 | convolution fusion | flops 56573820928 | bytes 76816384 | tf_op jit(solution)/shard_map/dot_general | solution.py:42
  677.8 12.6 constant_dynamic-slice_fusion
  690.4 0.0 all-gather.31.cloned.1.call-update
  690.4 0.0 reduce-scatter.7.cloned.1.call-start
  690.5 66.9 %convolution_convert_fusion = bf16[2048,8960]{1,0:T(8,128)(2,1)} fusion(bf16[1,1536,8960]{2,1,0:T(8,128)(2,1)} %all-gather.21.cloned.1.call-done, bf16[2048,1536]{0,1:T(8,128)(2,1)} %get-tuple-element.13, f32[2048]{0:T(1024)S(1)} %fusion.57), kind=kOutput, calls=%fused_computation.34 | convolution fusion | flops 56399233024 | bytes 70524928 | tf_op jit(solution)/shard_map/dot_general | solution.py:39
  757.4 105.4 %all-gather.25.cloned.1.call-done = bf16[1,8960,1536]{2,1,0:T(8,128)(2,1)} async-done(((bf16[1,4480,1536]{2,1,0:T(8,128)(2,1)}), bf16[1,8960,1536]{2,1,0:T(8,128)(2,1)}) %all-gather.25.cloned.1.call-update) | async-done | bytes 27525136 | tf_op jit(solution)/shard_map/all_gather | solution.py:49
  862.8 109.1 %fusion.7 = bf16[2048,8960]{1,0:T(8,128)(2,1)} fusion(bf16[2048,8960]{1,0:T(8,128)(2,1)} %convolution_convert_fusion, bf16[2048,1536]{1,0:T(8,128)(2,1)} %param.5, bf16[1,8960,1536]{2,1,0:T(8,128)(2,1)} %all-gather.25.cloned.1.call-done), kind=kOutput, calls=%fused_computation.18 | convolution fusion | flops 56793497600 | bytes 107216896 | tf_op jit(solution)/shard_map/dot_general | solution.py:51
  972.0 64.8 %fusion.50 = f32[1536,8960]{1,0:T(8,128)} fusion(bf16[2048,8960]{1,0:T(8,128)(2,1)} %fusion.7, bf16[2048,1536]{0,1:T(8,128)(2,1)S(1)} %copy-done, f32[2048]{0:T(1024)S(1)} %copy-done.7), kind=kOutput, calls=%fused_computation.74 | convolution fusion | flops 56380882944 | bytes 98050048 | tf_op jit(solution)/shard_map/dot_general | solution.py:54
  1036.7 0.0 reduce-scatter.7.cloned.1.call-update
  1036.8 0.0 reduce-scatter.5.cloned.1.call-start
  1036.8 8.8 copy.10
  1045.6 138.5 %all-gather.27.cloned.1.call-done = bf16[1,1536,8960]{2,1,0:T(8,128)(2,1)} async-done(((bf16[1,768,8960]{2,1,0:T(8,128)(2,1)}), bf16[1,1536,8960]{2,1,0:T(8,128)(2,1)}) %all-gather.27.cloned.1.call-update) | async-done | bytes 27525136 | tf_op jit(solution)/shard_map/all_gather | solution.py:48
  1184.1 79.0 %fusion.45 = (f32[2048]{0:T(1024)S(1)}, f32[2048,1536]{0,1:T(8,128)}) fusion(bf16[2048,1536]{0,1:T(8,128)(2,1)} %get-tuple-element.13, bf16[2048,8960]{1,0:T(8,128)(2,1)} %fusion.7, bf16[1,1536,8960]{2,1,0:T(8,128)(2,1)} %all-gather.27.cloned.1.call-done), kind=kOutput, calls=%fused_computation.73 | convolution fusion | flops 56380882944 | bytes 83107840 | tf_op jit(solution)/shard_map/dot_general | solution.py:55
  1263.1 12.6 fusion.35
  1275.6 229.2 %all-gather.29.cloned.1.call-done = bf16[1,8960,1536]{2,1,0:T(8,128)(2,1)} async-done(((bf16[1,4480,1536]{2,1,0:T(8,128)(2,1)}), bf16[1,8960,1536]{2,1,0:T(8,128)(2,1)}) %all-gather.29.cloned.1.call-update) | async-done | bytes 27525136 | tf_op jit(solution)/shard_map/all_gather | solution.py:49
  1504.9 119.0 %fusion.4 = bf16[2048,8960]{1,0:T(8,128)(2,1)} fusion(bf16[2048,8960]{1,0:T(8,128)(2,1)} %convolution_convert_fusion.1, bf16[2048,1536]{0,1:T(8,128)(2,1)} %fusion.35, bf16[1,8960,1536]{2,1,0:T(8,128)(2,1)} %all-gather.29.cloned.1.call-done), kind=kOutput, calls=%fused_computation.15 | convolution fusion | flops 56793497600 | bytes 107216896 | tf_op jit(solution)/shard_map/dot_general | solution.py:51
  1623.9 66.3 %fusion.53 = f32[1536,8960]{1,0:T(8,128)} fusion(bf16[2048,8960]{1,0:T(8,128)(2,1)} %fusion.4, bf16[2048,1536]{0,1:T(8,128)(2,1)} %copy.8, f32[2048]{0:T(1024)S(1)} %copy-done.4), kind=kOutput, calls=%fused_computation.75 | convolution fusion | flops 56380882944 | bytes 98050048 | tf_op jit(solution)/shard_map/dot_general | solution.py:54
  1690.2 0.0 reduce-scatter.5.cloned.1.call-update
  1690.2 0.0 reduce-scatter.11.cloned.1.call-start
  1690.2 82.0 %fusion.58 = f32[8960,1536]{1,0:T(8,128)} fusion(bf16[2048,1536]{1,0:T(8,128)(2,1)} %param.5, bf16[2048,8960]{1,0:T(8,128)(2,1)} %convolution_convert_fusion), kind=kOutput, calls=%fused_computation.86 | convolution fusion | flops 56554946560 | bytes 98041856 | tf_op jit(solution)/shard_map/dot_general | solution.py:50
  1772.2 0.0 reduce-scatter.11.cloned.1.call-update
  1772.2 0.0 reduce-scatter.9.cloned.1.call-start
  1772.3 85.1 %fusion.61 = f32[8960,1536]{1,0:T(8,128)} fusion(bf16[2048,1536]{0,1:T(8,128)(2,1)} %fusion.35, bf16[2048,8960]{1,0:T(8,128)(2,1)} %convolution_convert_fusion.1), kind=kOutput, calls=%fused_computation.87 | convolution fusion | flops 56554946560 | bytes 98041856 | tf_op jit(solution)/shard_map/dot_general | solution.py:50
  1857.4 0.0 reduce-scatter.9.cloned.1.call-update
  1857.4 71.8 %fusion.44 = bf16[2048,1536]{0,1:T(8,128)(2,1)} fusion(bf16[2048,1536]{0,1:T(8,128)(2,1)} %get-tuple-element.13, bf16[1,8960,1536]{2,1,0:T(8,128)(2,1)} %all-gather.23.cloned.1.call-done, bf16[2048,8960]{1,0:T(8,128)(2,1)} %convolution_convert_fusion), kind=kOutput, calls=%fused_computation.72 | convolution fusion | flops 56564383744 | bytes 76808192 | tf_op jit(solution)/shard_map/dot_general | solution.py:42
  1929.2 8.6 copy.12
  1937.9 74.0 %fusion.41 = (f32[2048]{0:T(1024)S(1)}, f32[2048,1536]{0,1:T(8,128)}) fusion(bf16[2048,1536]{0,1:T(8,128)(2,1)} %copy.8, bf16[2048,8960]{1,0:T(8,128)(2,1)} %fusion.4, bf16[1,1536,8960]{2,1,0:T(8,128)(2,1)} %all-gather.31.cloned.1.call-done), kind=kOutput, calls=%fused_computation.69 | convolution fusion | flops 56380882944 | bytes 83107840 | tf_op jit(solution)/shard_map/dot_general | solution.py:55
  2011.9 13.1 fusion.37
  2025.0 8.9 copy.13
  2033.9 100.9 %reduce-scatter.7.cloned.1.call-done = f32[192,8960]{1,0:T(8,128)} async-done(((f32[1536,8960]{1,0:T(8,128)}), f32[192,8960]{1,0:T(8,128)}) %reduce-scatter.7.cloned.1.call-update) | async-done | bytes 6881296 | tf_op jit(solution)/shard_map/reduce_scatter | solution.py:58
  2134.8 309.0 %reduce-scatter.5.cloned.1.call-done = f32[192,8960]{1,0:T(8,128)} async-done(((f32[1536,8960]{1,0:T(8,128)}), f32[192,8960]{1,0:T(8,128)}) %reduce-scatter.5.cloned.1.call-update) | async-done | bytes 6881296 | tf_op jit(solution)/shard_map/reduce_scatter | solution.py:58
  2443.8 13.0 pad_maximum_fusion
  2456.8 296.1 %reduce-scatter.11.cloned.1.call-done = f32[1120,1536]{1,0:T(8,128)} async-done(((f32[8960,1536]{1,0:T(8,128)}), f32[1120,1536]{1,0:T(8,128)}) %reduce-scatter.11.cloned.1.call-update) | async-done | bytes 6881296 | tf_op jit(solution)/shard_map/reduce_scatter | solution.py:59
  2752.8 309.0 %reduce-scatter.9.cloned.1.call-done = f32[1120,1536]{1,0:T(8,128)} async-done(((f32[8960,1536]{1,0:T(8,128)}), f32[1120,1536]{1,0:T(8,128)}) %reduce-scatter.9.cloned.1.call-update) | async-done | bytes 6881296 | tf_op jit(solution)/shard_map/reduce_scatter | solution.py:59
  3061.8 11.5 pad_maximum_fusion.1
  (23 shorter events, 0.1 us)
Async XLA Ops:
  7.2 139.0 %all-gather.23.cloned.1.call-start = ((), (), s32[]{:S(2)}) async-start(), calls=%async_computation.11 | async-start | bytes 30965760 | tf_op jit(solution)/shard_map/all_gather | solution.py:32
  13.6 264.6 %all-gather.21.cloned.1.call-start = ((), (), s32[]{:S(2)}) async-start(), calls=%async_computation.10 | async-start | bytes 30965760 | tf_op jit(solution)/shard_map/all_gather | solution.py:31
  20.0 390.2 %all-gather.19.cloned.1.call-start = ((), (), s32[]{:S(2)}) async-start(), calls=%async_computation.9 | async-start | bytes 30965760 | tf_op jit(solution)/shard_map/all_gather | solution.py:32
  20.8 520.8 %all-gather.17.cloned.1.call-start = ((), (), s32[]{:S(2)}) async-start(), calls=%async_computation.8 | async-start | bytes 30965760 | tf_op jit(solution)/shard_map/all_gather | solution.py:31
  21.3 841.4 %all-gather.25.cloned.1.call-start = ((), (), s32[]{:S(2)}) async-start(), calls=%async_computation.12 | async-start | bytes 41287680 | tf_op jit(solution)/shard_map/all_gather | solution.py:49
  159.1 1024.9 %all-gather.27.cloned.1.call-start = ((), (), s32[]{:S(2)}) async-start(), calls=%async_computation.13 | async-start | bytes 41287680 | tf_op jit(solution)/shard_map/all_gather | solution.py:48
  291.2 1213.7 %all-gather.29.cloned.1.call-start = ((), (), s32[]{:S(2)}) async-start(), calls=%async_computation.14 | async-start | bytes 41287680 | tf_op jit(solution)/shard_map/all_gather | solution.py:49
  423.3 1514.6 %all-gather.31.cloned.1.call-start = ((), (), s32[]{:S(2)}) async-start(), calls=%async_computation.15 | async-start | bytes 41287680 | tf_op jit(solution)/shard_map/all_gather | solution.py:48
  436.1 0.6 copy-start.1
  436.7 171.3 %copy-start.3 = (f32[2048]{0:T(1024)}, f32[2048]{0:T(1024)S(1)}, u32[]{:S(2)}) copy-start(f32[2048]{0:T(1024)S(1)} %fusion.56) | copy-start | bytes 24580
  677.8 79.6 %copy-start.8 = (f32[2048]{0:T(1024)}, f32[2048]{0:T(1024)S(1)}, u32[]{:S(2)}) copy-start(f32[2048]{0:T(1024)S(1)} %get-tuple-element.12) | copy-start | bytes 24580
  677.8 79.6 %copy-start.6 = (f32[2048]{0:T(1024)}, f32[2048]{0:T(1024)S(1)}, u32[]{:S(2)}) copy-start(f32[2048]{0:T(1024)S(1)} %fusion.57) | copy-start | bytes 24580
  690.4 1444.4 %reduce-scatter.7.cloned.1.call-start = ((), (), s32[]{:S(2)}) async-start(), calls=%async_computation.5 | async-start | bytes 61931520 | tf_op jit(solution)/shard_map/reduce_scatter | solution.py:58
  862.8 109.1 %copy-start = (bf16[2048,1536]{0,1:T(8,128)(2,1)S(1)}, bf16[2048,1536]{0,1:T(8,128)(2,1)}, u32[]{:S(2)}) copy-start(bf16[2048,1536]{0,1:T(8,128)(2,1)} %get-tuple-element.13) | copy-start | bytes 18874372
  862.8 109.2 %copy-start.7 = (f32[2048]{0:T(1024)S(1)}, f32[2048]{0:T(1024)}, u32[]{:S(2)}) copy-start(f32[2048]{0:T(1024)} %copy-done.6) | copy-start | bytes 24580
  1036.8 1407.0 %reduce-scatter.5.cloned.1.call-start = ((), (), s32[]{:S(2)}) async-start(), calls=%async_computation.4 | async-start | bytes 61931520 | tf_op jit(solution)/shard_map/reduce_scatter | solution.py:58
  1045.6 217.5 %copy-start.9 = (f32[2048]{0:T(1024)S(1)}, f32[2048]{0:T(1024)}, u32[]{:S(2)}) copy-start(f32[2048]{0:T(1024)} %copy-done.8) | copy-start | bytes 24580
  1504.9 119.0 %copy-start.4 = (f32[2048]{0:T(1024)S(1)}, f32[2048]{0:T(1024)}, u32[]{:S(2)}) copy-start(f32[2048]{0:T(1024)} %copy-done.3) | copy-start | bytes 24580
  1690.2 1062.7 %reduce-scatter.11.cloned.1.call-start = ((), (), s32[]{:S(2)}) async-start(), calls=%async_computation.7 | async-start | bytes 61931520 | tf_op jit(solution)/shard_map/reduce_scatter | solution.py:59
  1772.2 1289.6 %reduce-scatter.9.cloned.1.call-start = ((), (), s32[]{:S(2)}) async-start(), calls=%async_computation.6 | async-start | bytes 61931520 | tf_op jit(solution)/shard_map/reduce_scatter | solution.py:59
  1937.9 74.0 %copy-start.2 = (f32[2048]{0:T(1024)S(1)}, f32[2048]{0:T(1024)}, u32[]{:S(2)}) copy-start(f32[2048]{0:T(1024)} %copy-done.1) | copy-start | bytes 24580
  1937.9 74.0 %copy-start.5 = (f32[2048]{0:T(1024)S(1)}, f32[2048]{0:T(1024)}, u32[]{:S(2)}) copy-start(f32[2048]{0:T(1024)} %copy-done.3) | copy-start | bytes 24580
Sparse Core Ops, SparseCore 0:
  13.7 132.3 all-gather.22
  148.5 129.5 all-gather.20
  280.6 129.5 all-gather.18
  411.9 129.5 all-gather.16
  543.5 319.2 all-gather.24
  864.7 319.2 all-gather.26
  1185.6 319.2 all-gather.28
  1506.4 319.2 all-gather.30
  1829.3 305.4 reduce-scatter.6
  2138.2 305.5 reduce-scatter.4
  2447.3 305.4 reduce-scatter.10
  2756.2 305.5 reduce-scatter.8
where the time goes:
time: 3090 us; the launch traced here: 3080 us
  waiting for transfers between devices  1960 us (63%)
  matrix products  954 us (31%)
  local copies, waits for them, and re-layouts  99.9 us (3%)
  other arithmetic  54.3 us (2%)
    reduce_scatter x2, waiting for transfers between devices, device_fn(): lax.psum_scatter(down_part, BOTH_AXES, scatter_dimension=0, tiled=True)  605 us
    reduce_scatter x2, waiting for transfers between devices, device_fn(): lax.psum_scatter(up_part, BOTH_AXES, scatter_dimension=0, tiled=True)  410 us
    all_gather x2, waiting for transfers between devices, device_fn(): down_full = lax.all_gather(down_second, 'local', axis=0, tiled=True)  335 us
    all_gather x2, waiting for transfers between devices, device_fn(): down_full = lax.all_gather(w_down[layer_idx], BOTH_AXES, axis=0, tiled=True)  244 us
    dot_general x2, matrix products, device_fn(): lax.dot_general(cotangent, down_full, CONTRACT_COLS, preferred_element_ty...  228 us
    all_gather x2, waiting for transfers between devices, device_fn(): up_full = lax.all_gather(w_up[layer_idx], BOTH_AXES, axis=0, tiled=True)  224 us
    dot_general x2, matrix products, device_fn(): lax.dot_general(hidden, cotangent, CONTRACT_ROWS, preferred_element_type=...  167 us
    dot_general x2, matrix products, device_fn(): lax.dot_general(d_pre, up_full, CONTRACT_COLS, preferred_element_type=jnp...  153 us
  transfers between devices with their start and end apart: 12, of which 11 were waited for; matrix products, arithmetic and copies ran while one was open for 35% of the time, Pallas kernels for 0%

commit v1 on v0

v1 whole, which is shorter than its diff:
```python
import jax
import jax.numpy as jnp
from jax import lax
from jax.sharding import Mesh, PartitionSpec as P

NORM_EPS = 1e-6
ALL_AXES = ('y', 'x', 'core')
CHIPS = ('y', 'x')
SWAP = [(0, 1), (1, 0)]
CONTRACT_ROWS = (((0,), (0,)), ((), ()))
CONTRACT_COLS = (((1,), (1,)), ((), ()))
CONTRACT_MID = (((1,), (0,)), ((), ()))


def rms_norm(x_f32):
    return x_f32 * lax.rsqrt(jnp.mean(x_f32 * x_f32, axis=-1, keepdims=True) + NORM_EPS)


def gelu_tanh(values):
    return jax.nn.gelu(values, approximate=True)


def dot(a, b, dims=CONTRACT_MID):
    return lax.dot_general(a, b, dims, preferred_element_type=jnp.float32)


def partner(value):
    return lax.ppermute(value, 'core', SWAP)


def with_partner(value):
    return jnp.concatenate([value, partner(value)], axis=0)


def after(value, *others):
    return lax.optimization_barrier((value, *others))[0]


def solution(mesh):
    n_y = mesh.shape['local']
    n_x = mesh.shape['data'] // 2
    n_chips = n_y * n_x
    mesh3 = Mesh(mesh.devices.reshape(n_y, n_x, 2), ALL_AXES)
    tok_spec = P(ALL_AXES, None)
    w_spec = P(None, ALL_AXES, None)

    def device_fn(tokens, grad_out, w_up, w_down):
        even = lax.axis_index('core') == 0
        rows, _ = w_up.shape[1:]
        blk = w_down.shape[1]
        n_tok = tokens.shape[0]

        def pair_columns(w):
            even_cols = jnp.concatenate([w[:, (2 * k) * blk:(2 * k + 1) * blk] for k in range(n_chips)], axis=1)
            odd_cols = jnp.concatenate([w[:, (2 * k + 1) * blk:(2 * k + 2) * blk] for k in range(n_chips)], axis=1)
            mine = jnp.where(even, even_cols, odd_cols)
            other = partner(jnp.where(even, odd_cols, even_cols))
            return jnp.stack([jnp.where(even, mine, other), jnp.where(even, other, mine)])

        def chips_gather(value):
            return lax.all_gather(value, CHIPS, axis=0, tiled=False)

        def chips_scatter(value):
            return lax.psum_scatter(value, CHIPS, scatter_dimension=0, tiled=True)

        def half_sum(lhs, rhs, dims):
            theirs = partner(dot(lhs[n_tok:], rhs, dims))
            return dot(lhs[:n_tok], rhs, dims) + theirs

        def chips_gather_by_permute(value):
            top = value.shape[0] // 2
            from_x = lax.ppermute(value, 'x', SWAP)
            from_y = lax.ppermute(value, 'y', SWAP)
            diag = jnp.concatenate([lax.ppermute(from_x[:top], 'y', SWAP), lax.ppermute(from_y[top:], 'x', SWAP)])
            x_odd = lax.axis_index('x') == 1
            y_odd = lax.axis_index('y') == 1
            pair = [jnp.where(x_odd, p, q) for p, q in ((from_x, value), (value, from_x))]
            far = [jnp.where(x_odd, p, q) for p, q in ((diag, from_y), (from_y, diag))]
            return jnp.stack([jnp.where(y_odd, f, p) for p, f in zip(pair, far)] + [jnp.where(y_odd, p, f) for p, f in zip(pair, far)])

        def row_block(result):
            keep = jnp.where(even, result[:rows], result[rows:])
            recv = partner(jnp.where(even, result[rows:], result[:rows]))
            first = jnp.where(even, keep, recv)
            second = jnp.where(even, recv, keep)
            parts = []
            for k in range(n_chips):
                parts += [first[:, k * blk:(k + 1) * blk], second[:, k * blk:(k + 1) * blk]]
            return jnp.concatenate(parts, axis=1)

        def gelu_bwd(pre_act, d_hidden):
            _, back = jax.vjp(gelu_tanh, pre_act.astype(jnp.float32))
            return back(d_hidden.astype(jnp.float32))[0].astype(jnp.bfloat16)

        def norm_bwd(x, cotangent, d_normed):
            _, back = jax.vjp(rms_norm, x.astype(jnp.float32))
            return (cotangent.astype(jnp.float32) + back(d_normed)[0]).astype(jnp.bfloat16)

        def normed(x):
            return rms_norm(x.astype(jnp.float32)).astype(jnp.bfloat16)

        up0 = pair_columns(w_up[0])
        hid = n_chips * 2 * rows
        gat0 = chips_gather(up0)
        full_up0 = gat0.reshape(hid, -1)
        norm0 = with_partner(normed(tokens))
        up1 = pair_columns(after(w_up[1], up0, norm0))
        down0 = chips_gather(w_down[0]).reshape(n_chips * blk, -1)
        full_up1 = chips_gather(up1).reshape(hid, -1)
        down1 = chips_gather(w_down[1]).reshape(n_chips * blk, -1)

        pre0 = dot(norm0, full_up0).astype(jnp.bfloat16)
        kept0 = after(gat0[:, 0], pre0)
        hid0 = gelu_tanh(pre0.astype(jnp.float32)).astype(jnp.bfloat16)
        x1 = (tokens.astype(jnp.float32) + half_sum(hid0, down0, CONTRACT_MID)).astype(jnp.bfloat16)

        norm1 = with_partner(normed(x1))
        pre1 = dot(norm1, full_up1).astype(jnp.bfloat16)
        hid1 = gelu_tanh(pre1.astype(jnp.float32)).astype(jnp.bfloat16)
        g_pair = with_partner(grad_out)
        g_down1 = chips_scatter(dot(hid1, g_pair, CONTRACT_ROWS))
        again0 = chips_gather_by_permute(after(up0[1], pre1))

        d_hid1 = dot(g_pair, down1, CONTRACT_COLS).astype(jnp.bfloat16)
        d_pre1 = gelu_bwd(pre1, d_hid1)
        g_up1 = chips_scatter(dot(norm1, d_pre1, CONTRACT_ROWS))
        dx1 = norm_bwd(x1, grad_out, half_sum(d_pre1, full_up1, CONTRACT_COLS))

        dx1_pair = with_partner(dx1)
        d_hid0 = dot(dx1_pair, down0, CONTRACT_COLS).astype(jnp.bfloat16)
        d_pre0 = gelu_bwd(pre0, d_hid0)
        g_up0 = chips_scatter(dot(norm0, d_pre0, CONTRACT_ROWS))
        g_down0 = chips_scatter(dot(hid0, dx1_pair, CONTRACT_ROWS))
        x_out = (x1.astype(jnp.float32) + half_sum(hid1, down1, CONTRACT_MID)).astype(jnp.bfloat16)
        full_up0_again = jnp.stack([kept0, again0], axis=1).reshape(hid, -1)
        dx0 = norm_bwd(tokens, dx1, half_sum(d_pre0, full_up0_again, CONTRACT_COLS))

        blocks_up = [row_block(g_up0), row_block(g_up1)]
        grad_up = jnp.stack(blocks_up)
        grad_down = lax.optimization_barrier(jnp.stack([g_down1, g_down1]))
        grad_down = lax.dynamic_update_slice(grad_down, g_down0[None], (0, 0, 0))
        return x_out, dx0, grad_up, grad_down

    return jax.shard_map(device_fn, mesh=mesh3, in_specs=(tok_spec, tok_spec, w_spec, w_spec), out_specs=(tok_spec, tok_spec, w_spec, w_spec), check_vma=False)
```

time: 3090 us -> 1830 us (0.59)
  waiting for transfers between devices: 1960 us -> 639 us
  other arithmetic: 54.3 us -> 90.8 us
    reduce_scatter x4, waiting for transfers between devices: 1010 us -> 270 us  [chips_scatter(): return lax.psum_scatter(value, CHIPS, scatter_dimension=0, tiled=True)]
    all_gather x8 -> x4, waiting for transfers between devices: 941 us -> 265 us  [chips_gather(): return lax.all_gather(value, CHIPS, axis=0, tiled=False)]
    ppermute x0 -> x16, waiting for transfers between devices: none -> 105 us  [the longest x1 71.1 us: chips_gather_by_permute(): from_y = lax.ppermute(value, 'y', SWAP)]
    dynamic_slice x4 -> x0, local copies, waits for them, and re-layouts: 51.6 us -> none  [the longest x2 26 us: device_fn(): lax.dynamic_slice_in_dim(down_full, loc_index * down_rows, down_rows, axi...]
    dot_general x12 -> x16, matrix products: 954 us -> 984 us  [dot(): return lax.dot_general(a, b, dims, preferred_element_type=jnp.float32)]
  transfers between devices with their start and end apart: 12 -> 24, of which waited for: 11 -> 11; matrix products, arithmetic and copies ran while one was open for 35% -> 48% of each run, Pallas kernels for 0% -> 0%
where the time goes in v1:
time: 1830 us; the launch traced here: 1820 us
  matrix products  984 us (54%)
  waiting for transfers between devices  639 us (35%)
  other arithmetic  90.8 us (5%)
  local copies, waits for them, and re-layouts  87.1 us (5%)
    dot_general x16, matrix products, dot(): return lax.dot_general(a, b, dims, preferred_element_type=jnp.float32)  984 us
    reduce_scatter x4, waiting for transfers between devices, chips_scatter(): return lax.psum_scatter(value, CHIPS, scatter_dimension=0, tiled=True)  270 us
    all_gather x4, waiting for transfers between devices, chips_gather(): return lax.all_gather(value, CHIPS, axis=0, tiled=False)  265 us
    ppermute x1, waiting for transfers between devices, chips_gather_by_permute(): from_y = lax.ppermute(value, 'y', SWAP)  71.1 us
  transfers between devices with their start and end apart: 24, of which 11 were waited for; matrix products, arithmetic and copies ran while one was open for 48% of the time, Pallas kernels for 0%

profile of v1, /device:TPU:0, one launch (start us, length us, event | category | flops | bytes accessed | tf_op | source)
XLA Modules:
  0.0 1824.9 jit_solution(5697960976540173224)
XLA Ops:
  7.2 5.2 slice_bitcast_fusion.1
  12.4 2.5 fusion.75
  15.0 1.3 concatenate.34
  16.3 3.0 concatenate.35
  20.4 3.2 collective-permute-done.1
  25.4 2.1 pad_maximum_fusion.10
  27.5 4.2 fusion.42
  32.4 8.7 fusion.43
  41.5 3.3 fusion.69
  45.2 6.4 collective-permute-done
  51.6 105.0 %all-gather.11.cloned.1.call-done = bf16[8,192,4480]{2,1,0:T(8,128)(2,1)} async-done(((bf16[2,192,4480]{2,1,0:T(8,128)(2,1)}), bf16[8,192,4480]{2,1,0:T(8,128)(2,1)}) %all-gather.11.cloned.1.call-update) | async-done | bytes 13762576 | tf_op jit(solution)/shard_map/all_gather | solution.py:61
  156.6 80.7 %fusion.13 = (bf16[4096,4480]{1,0:T(8,128)(2,1)}, bf16[4096,4480]{1,0:T(8,128)(2,1)}) fusion(bf16[1536,4480]{1,0:T(8,128)(2,1)} %bitcast.68, bf16[2048,1536]{1,0:T(8,128)(2,1)} %collective-permute-done, bf16[2048,1536]{1,0:T(8,128)(2,1)} %fusion.43), kind=kOutput, calls=%fused_computation.25 | convolution fusion | flops 56598462464 | bytes 99745792 | tf_op jit(solution)/shard_map/dot_general | solution.py:24
  237.4 48.3 %all-gather.7.cloned.1.call-done = bf16[4,1120,1536]{2,1,0:T(8,128)(2,1)} async-done(((bf16[1,1120,1536]{2,1,0:T(8,128)(2,1)}), bf16[4,1120,1536]{2,1,0:T(8,128)(2,1)}) %all-gather.7.cloned.1.call-update) | async-done | bytes 13762576 | tf_op jit(solution)/shard_map/all_gather | solution.py:61
  285.6 38.4 %fusion.34 = f32[2048,1536]{1,0:T(8,128)} fusion(bf16[4480,1536]{1,0:T(8,128)(2,1)} %bitcast.73, bf16[4096,4480]{1,0:T(8,128)(2,1)} %get-tuple-element.58), kind=kOutput, calls=%fused_computation.62 | convolution fusion | flops 28185722880 | bytes 44695552 | tf_op jit(solution)/shard_map/dot_general | solution.py:24
  324.1 2.6 fusion.74
  328.0 3.0 concatenate.38
  331.8 14.2 collective-permute-done.4
  346.4 2.1 pad_maximum_fusion.11
  348.7 42.3 %fusion.46 = (f32[2048]{0:T(1024)S(1)}, bf16[2048,1536]{1,0:T(8,128)(2,1)S(1)}) fusion(f32[2048,1536]{1,0:T(8,128)} %collective-permute-done.2, bf16[4480,1536]{1,0:T(8,128)(2,1)} %bitcast.74, bf16[4096,4480]{1,0:T(8,128)(2,1)} %get-tuple-element.58, bf16[2048,1536]{1,0:T(8,128)(2,1)} %param.4), kind=kOutput, calls=%fused_computation.77 | convolution fusion | flops 28207740928 | bytes 57286656 | tf_op jit(solution)/shard_map/dot_general | solution.py:24
  391.0 2.7 copy-done.2
  393.7 3.8 fusion.47
  397.9 7.3 constant_dynamic-update-slice_fusion.1
  405.2 5.9 constant_dynamic-update-slice_fusion
  411.1 64.2 %all-gather.13.cloned.1.call-done = bf16[8,192,4480]{2,1,0:T(8,128)(2,1)} async-done(((bf16[2,192,4480]{2,1,0:T(8,128)(2,1)}), bf16[8,192,4480]{2,1,0:T(8,128)(2,1)}) %all-gather.13.cloned.1.call-update) | async-done | bytes 13762576 | tf_op jit(solution)/shard_map/all_gather | solution.py:61
  475.3 81.2 %fusion.19 = (bf16[4096,4480]{1,0:T(8,128)(2,1)}, bf16[4096,4480]{1,0:T(8,128)(2,1)}) fusion(bf16[1536,4480]{1,0:T(8,128)(2,1)} %bitcast.76, bf16[2048,1536]{1,0:T(8,128)(2,1)} %collective-permute-done.3, bf16[2048,1536]{1,0:T(8,128)(2,1)} %fusion.47), kind=kOutput, calls=%fused_computation.31 | convolution fusion | flops 56598462464 | bytes 99745792 | tf_op jit(solution)/shard_map/dot_general | solution.py:24
  556.5 47.1 %all-gather.9.cloned.1.call-done = bf16[4,1120,1536]{2,1,0:T(8,128)(2,1)} async-done(((bf16[1,1120,1536]{2,1,0:T(8,128)(2,1)}), bf16[4,1120,1536]{2,1,0:T(8,128)(2,1)}) %all-gather.9.cloned.1.call-update) | async-done | bytes 13762576 | tf_op jit(solution)/shard_map/all_gather | solution.py:61
  603.6 115.0 %fusion.4 = bf16[4096,4480]{1,0:T(8,128)(2,1)} fusion(bf16[4096,4480]{1,0:T(8,128)(2,1)} %get-tuple-element.63, bf16[4096,1536]{1,0:T(8,128)(2,1)} %constant_dynamic-update-slice_fusion, bf16[4480,1536]{1,0:T(8,128)(2,1)} %bitcast.70), kind=kOutput, calls=%fused_computation.16 | convolution fusion | flops 56793497600 | bytes 99745792 | tf_op jit(solution)/shard_map/dot_general | solution.py:24
  718.6 71.2 %fusion.61 = f32[1536,4480]{1,0:T(8,128)} fusion(bf16[4096,4480]{1,0:T(8,128)(2,1)} %fusion.4, bf16[2048,1536]{1,0:T(8,128)(2,1)} %collective-permute-done.3, bf16[2048,1536]{1,0:T(8,128)(2,1)} %fusion.47), kind=kOutput, calls=%fused_computation.87 | convolution fusion | flops 56396611584 | bytes 76808192 | tf_op jit(solution)/shard_map/dot_general | solution.py:24
  789.9 39.3 %fusion.26 = f32[2048,1536]{1,0:T(8,128)} fusion(bf16[1536,4480]{1,0:T(8,128)(2,1)} %bitcast.77, bf16[4096,4480]{1,0:T(8,128)(2,1)} %fusion.4), kind=kOutput, calls=%fused_computation.54 | convolution fusion | flops 28185722880 | bytes 44695552 | tf_op jit(solution)/shard_map/dot_general | solution.py:24
  829.2 68.2 %fusion.76 = f32[4480,1536]{1,0:T(8,128)} fusion(bf16[4096,4480]{1,0:T(8,128)(2,1)} %get-tuple-element.62, bf16[4096,1536]{1,0:T(8,128)(2,1)} %constant_dynamic-update-slice_fusion), kind=kOutput, calls=%fused_computation.141 | convolution fusion | flops 56371445760 | bytes 76808192 | tf_op jit(solution)/shard_map/dot_general | solution.py:24
  897.4 40.2 %fusion.49 = (f32[2048]{0:T(1024)S(1)}, f32[2048,1536]{1,0:T(8,128)}) fusion(bf16[2048,1536]{1,0:T(8,128)(2,1)} %copy-done.2, f32[2048,1536]{1,0:T(8,128)} %collective-permute-done.7, bf16[1536,4480]{1,0:T(8,128)(2,1)} %bitcast.78, bf16[4096,4480]{1,0:T(8,128)(2,1)} %fusion.4), kind=kOutput, calls=%fused_computation.80 | convolution fusion | flops 28198303744 | bytes 63578112 | tf_op jit(solution)/shard_map/dot_general | solution.py:24
  937.7 9.9 fusion.39
  947.6 2.6 copy-done.1
  950.4 10.0 collective-permute-done.8
  960.4 2.7 copy-done.14
  963.1 110.7 %fusion.7 = bf16[4096,4480]{1,0:T(8,128)(2,1)} fusion(bf16[4096,4480]{1,0:T(8,128)(2,1)} %get-tuple-element.59, bf16[4480,1536]{1,0:T(8,128)(2,1)} %bitcast.75, bf16[2048,1536]{1,0:T(8,128)(2,1)} %copy-done.14, bf16[2048,1536]{1,0:T(8,128)(2,1)} %copy-done.1), kind=kOutput, calls=%fused_computation.19 | convolution fusion | flops 56818663424 | bytes 99745792 | tf_op jit(solution)/shard_map/dot_general | solution.py:24
  1073.8 71.6 %fusion.68 = f32[1536,4480]{1,0:T(8,128)} fusion(bf16[4096,4480]{1,0:T(8,128)(2,1)} %fusion.7, bf16[2048,1536]{1,0:T(8,128)(2,1)} %collective-permute-done, bf16[2048,1536]{1,0:T(8,128)(2,1)} %fusion.43), kind=kOutput, calls=%fused_computation.133 | convolution fusion | flops 56396611584 | bytes 76808192 | tf_op jit(solution)/shard_map/dot_general | solution.py:24
  1145.4 68.5 %fusion.60 = f32[4480,1536]{1,0:T(8,128)} fusion(bf16[4096,4480]{1,0:T(8,128)(2,1)} %get-tuple-element.58, bf16[2048,1536]{1,0:T(8,128)(2,1)} %copy-done.14, bf16[2048,1536]{1,0:T(8,128)(2,1)} %copy-done.1), kind=kOutput, calls=%fused_computation.86 | convolution fusion | flops 56396611584 | bytes 76808192 | tf_op jit(solution)/shard_map/dot_general | solution.py:24
  1213.9 1.4 copy-done.4
  1215.4 1.6 collective-permute-start.11
  1217.8 3.4 slice_bitcast_fusion
  1221.3 71.1 %collective-permute-done.11 = bf16[192,4480]{1,0:T(8,128)(2,1)S(1)} collective-permute-done((bf16[192,4480]{1,0:T(8,128)(2,1)S(1)}, bf16[192,4480]{1,0:T(8,128)(2,1)S(1)}, u32[]{:S(2)}, u32[]{:S(2)}) %collective-permute-start.11) | collective-permute-done | bytes 1720352 | tf_op jit(solution)/shard_map/ppermute | solution.py:73
  1292.4 1.7 collective-permute-start.12
  1296.2 38.0 %fusion.30 = f32[2048,1536]{1,0:T(8,128)} fusion(bf16[4480,1536]{1,0:T(8,128)(2,1)} %bitcast.71, bf16[4096,4480]{1,0:T(8,128)(2,1)} %get-tuple-element.62), kind=kOutput, calls=%fused_computation.58 | convolution fusion | flops 28185722880 | bytes 44695552 | tf_op jit(solution)/shard_map/dot_general | solution.py:24
  1334.4 2.1 select_bitcast_fusion.3
  1337.6 1.6 pad_maximum_fusion
  1339.1 5.8 copy.13
  1344.9 38.8 %fusion.22 = f32[2048,1536]{1,0:T(8,128)} fusion(bf16[1536,4480]{1,0:T(8,128)(2,1)} %bitcast.63, bf16[4096,4480]{1,0:T(8,128)(2,1)} %fusion.7), kind=kOutput, calls=%fused_computation.50 | convolution fusion | flops 28185722880 | bytes 44695552 | tf_op jit(solution)/shard_map/dot_general | solution.py:24
  1384.2 40.3 %fusion.48 = bf16[2048,1536]{1,0:T(8,128)(2,1)} fusion(bf16[2048,1536]{1,0:T(8,128)(2,1)} %copy-done.2, f32[2048,1536]{1,0:T(8,128)} %collective-permute-done.5, bf16[4480,1536]{1,0:T(8,128)(2,1)} %bitcast.72, bf16[4096,4480]{1,0:T(8,128)(2,1)} %get-tuple-element.62), kind=kOutput, calls=%fused_computation.79 | convolution fusion | flops 28198305792 | bytes 57278464 | tf_op jit(solution)/shard_map/dot_general | solution.py:24
  1424.6 39.7 %fusion.45 = (f32[2048]{0:T(1024)S(1)}, f32[2048,1536]{1,0:T(8,128)}) fusion(bf16[2048,1536]{1,0:T(8,128)(2,1)} %param.4, f32[2048,1536]{1,0:T(8,128)} %collective-permute-done.13, bf16[1536,4480]{1,0:T(8,128)(2,1)} %bitcast.64, bf16[4096,4480]{1,0:T(8,128)(2,1)} %fusion.7), kind=kOutput, calls=%fused_computation.76 | convolution fusion | flops 28198303744 | bytes 63578112 | tf_op jit(solution)/shard_map/dot_general | solution.py:24
  1464.3 5.6 slice_select_fusion
  1470.6 11.3 fusion.41
  1481.9 11.7 pad_maximum_fusion.2
  1493.7 52.7 %reduce-scatter.5.cloned.1.call-done = f32[384,4480]{1,0:T(8,128)} async-done(((f32[1536,4480]{1,0:T(8,128)}), f32[384,4480]{1,0:T(8,128)}) %reduce-scatter.5.cloned.1.call-update) | async-done | bytes 6881296 | tf_op jit(solution)/shard_map/reduce_scatter | solution.py:64
  1546.4 5.1 slice_select_fusion.2
  1551.6 4.8 broadcast_select_fusion.4
  1556.3 3.2 fusion.72
  1559.6 8.2 concatenate.43
  1567.7 217.0 %reduce-scatter.11.cloned.1.call-done = f32[1120,1536]{1,0:T(8,128)} async-done(((f32[4480,1536]{1,0:T(8,128)}), f32[1120,1536]{1,0:T(8,128)}) %reduce-scatter.11.cloned.1.call-update) | async-done | bytes 6881296 | tf_op jit(solution)/shard_map/reduce_scatter | solution.py:64
  1784.7 6.4 bitcast_dynamic-update-slice_fusion
  1791.1 4.6 broadcast_select_fusion.6
  1795.7 3.2 fusion.70
  1798.9 7.9 concatenate.42
  1806.9 11.0 pad_maximum_fusion.1
  (88 shorter events, 13.1 us)
Async XLA Ops:
  7.2 149.5 %all-gather.11.cloned.1.call-start = ((), (), s32[]{:S(2)}) async-start(), calls=%async_computation.10 | async-start | bytes 17203200 | tf_op jit(solution)/shard_map/all_gather | solution.py:61
  19.6 4.1 collective-permute-start.1
  24.1 1.3 copy-start.3
  27.5 14.0 slice-start
  27.5 258.2 %all-gather.7.cloned.1.call-start = ((), (), s32[]{:S(2)}) async-start(), calls=%async_computation.4 | async-start | bytes 17203200 | tf_op jit(solution)/shard_map/all_gather | solution.py:61
  31.8 0.6 copy-start.6
  32.4 12.4 copy-start.8
  32.4 9.1 slice-start.1
  41.1 10.5 collective-permute-start
  44.9 430.4 %all-gather.13.cloned.1.call-start = ((), (), s32[]{:S(2)}) async-start(), calls=%async_computation.11 | async-start | bytes 17203200 | tf_op jit(solution)/shard_map/all_gather | solution.py:61
  285.6 38.5 %copy-start.5 = (bf16[192,8960]{1,0:T(8,128)(2,1)S(1)}, bf16[192,8960]{1,0:T(8,128)(2,1)}, u32[]{:S(2)}) copy-start(bf16[192,8960]{1,0:T(8,128)(2,1)} %get-tuple-element.7) | copy-start | bytes 10321924
  324.1 24.6 %collective-permute-start.2 = (f32[2048,1536]{1,0:T(8,128)}, f32[2048,1536]{1,0:T(8,128)}, u32[]{:S(2)}, u32[]{:S(2)}) collective-permute-start(f32[2048,1536]{1,0:T(8,128)} %fusion.34), channel_id=1, source_target_pairs={{0,1},{1,0},{2,3},{3,2},{4,5},{5,4},{6,7},{7,6}} | collective-permute-start | bytes 37748744 | tf_op jit(solution)/shard_map/ppermute | solution.py:28
  331.3 14.7 collective-permute-start.4
  348.5 255.1 %all-gather.9.cloned.1.call-start = ((), (), s32[]{:S(2)}) async-start(), calls=%async_computation.5 | async-start | bytes 17203200 | tf_op jit(solution)/shard_map/all_gather | solution.py:61
  348.5 56.7 %collective-permute-start.6 = (bf16[2048,1536]{1,0:T(8,128)(2,1)}, bf16[2048,1536]{1,0:T(8,128)(2,1)}, u32[]{:S(2)}, u32[]{:S(2)}) collective-permute-start(bf16[2048,1536]{1,0:T(8,128)(2,1)} %param.5), channel_id=1, source_target_pairs={{0,1},{1,0},{2,3},{3,2},{4,5},{5,4},{6,7},{7,6}} | collective-permute-start | bytes 18874376 | tf_op jit(solution)/shard_map/ppermute | solution.py:28
  391.0 2.7 copy-start.2
  391.0 6.8 copy-start.12
  391.0 6.5 copy-start.10
  397.5 77.8 %collective-permute-start.3 = (bf16[2048,1536]{1,0:T(8,128)(2,1)}, bf16[2048,1536]{1,0:T(8,128)(2,1)}, u32[]{:S(2)}, u32[]{:S(2)}) collective-permute-start(bf16[2048,1536]{1,0:T(8,128)(2,1)} %fusion.47), channel_id=1, source_target_pairs={{0,1},{1,0},{2,3},{3,2},{4,5},{5,4},{6,7},{7,6}} | collective-permute-start | bytes 18874376 | tf_op jit(solution)/shard_map/ppermute | solution.py:28
  397.9 1066.4 %reduce-scatter.7.cloned.1.call-start = ((), (), s32[]{:S(2)}) async-start(), calls=%async_computation.7 | async-start | bytes 34406400 | tf_op jit(solution)/shard_map/reduce_scatter | solution.py:64
  789.9 692.1 %reduce-scatter.9.cloned.1.call-start = ((), (), s32[]{:S(2)}) async-start(), calls=%async_computation.8 | async-start | bytes 34406400 | tf_op jit(solution)/shard_map/reduce_scatter | solution.py:64
  829.2 68.3 %collective-permute-start.7 = (f32[2048,1536]{1,0:T(8,128)}, f32[2048,1536]{1,0:T(8,128)}, u32[]{:S(2)}, u32[]{:S(2)}) collective-permute-start(f32[2048,1536]{1,0:T(8,128)} %fusion.26), channel_id=1, source_target_pairs={{0,1},{1,0},{2,3},{3,2},{4,5},{5,4},{6,7},{7,6}} | collective-permute-start | bytes 37748744 | tf_op jit(solution)/shard_map/ppermute | solution.py:28
  897.4 40.3 %copy-start.13 = (f32[2048]{0:T(1024)S(1)}, f32[2048]{0:T(1024)}, u32[]{:S(2)}) copy-start(f32[2048]{0:T(1024)} %copy-done.12) | copy-start | bytes 24580
  897.4 40.3 %copy-start.11 = (f32[2048]{0:T(1024)S(1)}, f32[2048]{0:T(1024)}, u32[]{:S(2)}) copy-start(f32[2048]{0:T(1024)} %copy-done.10) | copy-start | bytes 24580
  897.4 649.0 %reduce-scatter.5.cloned.1.call-start = ((), (), s32[]{:S(2)}) async-start(), calls=%async_computation.6 | async-start | bytes 34406400 | tf_op jit(solution)/shard_map/reduce_scatter | solution.py:64
  947.6 2.6 copy-start.1
  950.2 10.2 collective-permute-start.8
  960.4 2.7 copy-start.14
  1145.4 639.3 %reduce-scatter.11.cloned.1.call-start = ((), (), s32[]{:S(2)}) async-start(), calls=%async_computation.9 | async-start | bytes 34406400 | tf_op jit(solution)/shard_map/reduce_scatter | solution.py:64
  1213.9 1.5 copy-start.4
  1215.4 77.0 %collective-permute-start.11 = (bf16[192,4480]{1,0:T(8,128)(2,1)S(1)}, bf16[192,4480]{1,0:T(8,128)(2,1)S(1)}, u32[]{:S(2)}, u32[]{:S(2)}) collective-permute-start(bf16[192,4480]{1,0:T(8,128)(2,1)S(1)} %copy-done.4), channel_id=1, source_target_pairs={{0,4},{4,0},{1,5},{5,1},{2,6},{6,2},{3,7},{7,3}} | collective-permute-start | bytes 5160968 | tf_op jit(solution)/shard_map/ppermute | solution.py:73
  1217.0 77.0 %collective-permute-start.9 = (bf16[192,4480]{1,0:T(8,128)(2,1)S(1)}, bf16[192,4480]{1,0:T(8,128)(2,1)}, u32[]{:S(2)}, u32[]{:S(2)}) collective-permute-start(bf16[192,4480]{1,0:T(8,128)(2,1)S(1)} %copy-done.4), channel_id=1, source_target_pairs={{0,2},{2,0},{1,3},{3,1},{4,6},{6,4},{5,7},{7,5}} | collective-permute-start | bytes 5160968 | tf_op jit(solution)/shard_map/ppermute | solution.py:72
  1292.4 41.9 %collective-permute-start.12 = (bf16[96,4480]{1,0:T(8,128)(2,1)S(1)}, bf16[96,4480]{1,0:T(8,128)(2,1)S(1)}, u32[]{:S(2)}, u32[]{:S(2)}) collective-permute-start(bf16[96,4480]{1,0:T(8,128)(2,1)S(1)} %slice.225), channel_id=1, source_target_pairs={{0,2},{2,0},{1,3},{3,1},{4,6},{6,4},{5,7},{7,5}} | collective-permute-start | bytes 2580488 | tf_op jit(solution)/shard_map/ppermute | solution.py:74
  1295.3 38.9 %collective-permute-start.10 = (bf16[96,4480]{1,0:T(8,128)(2,1)S(1)}, bf16[96,4480]{1,0:T(8,128)(2,1)S(1)}, u32[]{:S(2)}, u32[]{:S(2)}) collective-permute-start(bf16[96,4480]{1,0:T(8,128)(2,1)S(1)} %slice.224), channel_id=1, source_target_pairs={{0,4},{4,0},{1,5},{5,1},{2,6},{6,2},{3,7},{7,3}} | collective-permute-start | bytes 2580488 | tf_op jit(solution)/shard_map/ppermute | solution.py:74
  1334.2 50.0 %collective-permute-start.5 = (f32[2048,1536]{1,0:T(8,128)}, f32[2048,1536]{1,0:T(8,128)}, u32[]{:S(2)}, u32[]{:S(2)}) collective-permute-start(f32[2048,1536]{1,0:T(8,128)} %fusion.30), channel_id=1, source_target_pairs={{0,1},{1,0},{2,3},{3,2},{4,5},{5,4},{6,7},{7,6}} | collective-permute-start | bytes 37748744 | tf_op jit(solution)/shard_map/ppermute | solution.py:28
  1383.8 40.8 %collective-permute-start.13 = (f32[2048,1536]{1,0:T(8,128)}, f32[2048,1536]{1,0:T(8,128)}, u32[]{:S(2)}, u32[]{:S(2)}) collective-permute-start(f32[2048,1536]{1,0:T(8,128)} %fusion.22), channel_id=1, source_target_pairs={{0,1},{1,0},{2,3},{3,2},{4,5},{5,4},{6,7},{7,6}} | collective-permute-start | bytes 37748744 | tf_op jit(solution)/shard_map/ppermute | solution.py:28
  1424.6 39.7 %copy-start.7 = (f32[2048]{0:T(1024)S(1)}, f32[2048]{0:T(1024)}, u32[]{:S(2)}) copy-start(f32[2048]{0:T(1024)} %copy-done.6) | copy-start | bytes 24580
  1424.6 45.5 %copy-start.9 = (f32[2048]{0:T(1024)S(1)}, f32[2048]{0:T(1024)}, u32[]{:S(2)}) copy-start(f32[2048]{0:T(1024)} %copy-done.8) | copy-start | bytes 24580
  1464.3 6.3 copy-start
  1469.9 81.7 %collective-permute-start.15 = (f32[192,4480]{1,0:T(8,128)}, f32[192,4480]{1,0:T(8,128)S(1)}, u32[]{:S(2)}, u32[]{:S(2)}) collective-permute-start(f32[192,4480]{1,0:T(8,128)} %slice_select_fusion), channel_id=1, source_target_pairs={{0,1},{1,0},{2,3},{3,2},{4,5},{5,4},{6,7},{7,6}} | collective-permute-start | bytes 10321928 | tf_op jit(solution)/shard_map/ppermute | solution.py:28
  1551.6 239.6 %collective-permute-start.14 = (f32[192,4480]{1,0:T(8,128)}, f32[192,4480]{1,0:T(8,128)}, u32[]{:S(2)}, u32[]{:S(2)}) collective-permute-start(f32[192,4480]{1,0:T(8,128)} %slice_select_fusion.2), channel_id=1, source_target_pairs={{0,1},{1,0},{2,3},{3,2},{4,5},{5,4},{6,7},{7,6}} | collective-permute-start | bytes 10321928 | tf_op jit(solution)/shard_map/ppermute | solution.py:28
Sparse Core Ops, SparseCore 0:
  27.6 128.9 all-gather.10
  159.0 126.6 all-gather.6
  348.6 126.6 all-gather.12
  476.9 126.6 all-gather.8
  790.0 235.2 reduce-scatter.6
  1028.2 275.9 reduce-scatter.8
  1307.2 239.1 reduce-scatter.4
  1549.4 235.2 reduce-scatter.10

commit v2 on v1

v2 whole, which is shorter than its diff:
```python
import jax
import jax.numpy as jnp
from jax import lax
from jax.experimental import pallas as pl
from jax.sharding import Mesh, PartitionSpec as P

NORM_EPS = 1e-6
ROW_TILE = 32
PIECES = 2
ALL_AXES = ('y', 'x', 'core')
CHIPS = ('y', 'x')
SWAP = [(0, 1), (1, 0)]
CONTRACT_ROWS = (((0,), (0,)), ((), ()))
CONTRACT_COLS = (((1,), (1,)), ((), ()))
CONTRACT_MID = (((1,), (0,)), ((), ()))


def rms_norm(x_f32):
    return x_f32 * lax.rsqrt(jnp.mean(x_f32 * x_f32, axis=-1, keepdims=True) + NORM_EPS)


def gelu_tanh(values):
    return jax.nn.gelu(values, approximate=True)


def dot(a, b, dims=CONTRACT_MID):
    return lax.dot_general(a, b, dims, preferred_element_type=jnp.float32)


def partner(value):
    return lax.ppermute(value, 'core', SWAP)


def with_partner(value):
    return jnp.concatenate([value, partner(value)], axis=0)


def after(value, *others):
    return lax.optimization_barrier((value, *others))[0]


def solution(mesh):
    n_y = mesh.shape['local']
    n_x = mesh.shape['data'] // 2
    n_chips = n_y * n_x
    mesh3 = Mesh(mesh.devices.reshape(n_y, n_x, 2), ALL_AXES)
    tok_spec = P(ALL_AXES, None)
    w_spec = P(None, ALL_AXES, None)

    def device_fn(tokens, grad_out, w_up, w_down):
        even = lax.axis_index('core') == 0
        rows, ffn = w_up.shape[1:]
        blk = w_down.shape[1]
        n_tok = tokens.shape[0]

        def pick(layer):
            def kernel(w_ref, mine_ref, other_ref):
                is_even = lax.axis_index('core') == 0

                def copy(first, mine, other):
                    for k in range(n_chips):
                        dst = slice(k * blk, (k + 1) * blk)
                        mine[:, dst] = w_ref[:, (2 * k + first) * blk:(2 * k + first + 1) * blk]
                        other[:, dst] = w_ref[:, (2 * k + 1 - first) * blk:(2 * k + 2 - first) * blk]

                @pl.when(is_even)
                def _():
                    copy(0, mine_ref, other_ref)

                @pl.when(jnp.logical_not(is_even))
                def _():
                    copy(1, mine_ref, other_ref)

            half = jax.ShapeDtypeStruct((rows, ffn // 2), w_up.dtype)
            spec = pl.BlockSpec((ROW_TILE, ffn // 2), lambda i: (i, 0))
            return pl.pallas_call(
                kernel, grid=(rows // ROW_TILE,), out_shape=(half, half),
                in_specs=[pl.BlockSpec((None, ROW_TILE, ffn), lambda i: (layer, i, 0))], out_specs=(spec, spec), name='pick')

        def join(mine, other):
            def kernel(mine_ref, other_ref, out_ref):
                is_even = lax.axis_index('core') == 0

                @pl.when(is_even)
                def _():
                    out_ref[0] = mine_ref[...]
                    out_ref[1] = other_ref[...]

                @pl.when(jnp.logical_not(is_even))
                def _():
                    out_ref[0] = other_ref[...]
                    out_ref[1] = mine_ref[...]

            spec = pl.BlockSpec((ROW_TILE, ffn // 2), lambda i: (i, 0))
            return pl.pallas_call(
                kernel, grid=(rows // ROW_TILE,), out_shape=jax.ShapeDtypeStruct((2, rows, ffn // 2), w_up.dtype),
                in_specs=[spec, spec], out_specs=pl.BlockSpec((2, ROW_TILE, ffn // 2), lambda i: (0, i, 0)), name='join')(mine, other)

        def pair_columns(w, layer):
            mine, other = pick(layer)(w)
            return join(mine, partner(other))

        whole_spec = pl.BlockSpec((1, 2, ROW_TILE, ffn // 2), lambda c, i: (c, 0, i, 0))
        part_spec = pl.BlockSpec((1, ROW_TILE, ffn // 2), lambda c, i: (c, i, 0))
        part_shape = jax.ShapeDtypeStruct((n_chips, rows, ffn // 2), w_up.dtype)
        part_grid = (n_chips, rows // ROW_TILE)

        def split(whole):
            def kernel(whole_ref, keep_ref, give_ref):
                is_even = lax.axis_index('core') == 0

                @pl.when(is_even)
                def _():
                    keep_ref[...] = whole_ref[:, 0]
                    give_ref[...] = whole_ref[:, 1]

                @pl.when(jnp.logical_not(is_even))
                def _():
                    keep_ref[...] = whole_ref[:, 1]
                    give_ref[...] = whole_ref[:, 0]

            return pl.pallas_call(kernel, grid=part_grid, out_shape=(part_shape, part_shape), in_specs=[whole_spec], out_specs=(part_spec, part_spec), name='split')(whole)

        def merge(kept, taken):
            def kernel(keep_ref, take_ref, whole_ref):
                is_even = lax.axis_index('core') == 0

                @pl.when(is_even)
                def _():
                    whole_ref[:, 0] = keep_ref[...]
                    whole_ref[:, 1] = take_ref[...]

                @pl.when(jnp.logical_not(is_even))
                def _():
                    whole_ref[:, 0] = take_ref[...]
                    whole_ref[:, 1] = keep_ref[...]

            shape = jax.ShapeDtypeStruct((n_chips, 2, rows, ffn // 2), w_up.dtype)
            return pl.pallas_call(kernel, grid=part_grid, out_shape=shape, in_specs=[part_spec, part_spec], out_specs=whole_spec, name='merge')(kept, taken)

        def chips_gather(value):
            return lax.all_gather(value, CHIPS, axis=0, tiled=False)

        def chips_scatter(value):
            return lax.psum_scatter(value, CHIPS, scatter_dimension=0, tiled=True)

        def half_sum(lhs, rhs, dims, pieces=1):
            step = n_tok // pieces
            theirs = [partner(dot(lhs[n_tok + i * step:n_tok + (i + 1) * step], rhs, dims)) for i in range(pieces)]
            return [dot(lhs[i * step:(i + 1) * step], rhs, dims) + theirs[i] for i in range(pieces)]

        def row_block(result):
            keep = jnp.where(even, result[:rows], result[rows:])
            recv = partner(jnp.where(even, result[rows:], result[:rows]))
            first = jnp.where(even, keep, recv)
            second = jnp.where(even, recv, keep)
            parts = []
            for k in range(n_chips):
                parts += [first[:, k * blk:(k + 1) * blk], second[:, k * blk:(k + 1) * blk]]
            return jnp.concatenate(parts, axis=1)

        def gelu_bwd(pre_act, d_hidden):
            _, back = jax.vjp(gelu_tanh, pre_act.astype(jnp.float32))
            return back(d_hidden.astype(jnp.float32))[0].astype(jnp.bfloat16)

        def norm_bwd(x, cotangent, d_normed):
            _, back = jax.vjp(rms_norm, x.astype(jnp.float32))
            return (cotangent.astype(jnp.float32) + back(d_normed)[0]).astype(jnp.bfloat16)

        def normed(x):
            return rms_norm(x.astype(jnp.float32)).astype(jnp.bfloat16)

        up0 = pair_columns(w_up, 0)
        hid = n_chips * 2 * rows
        gat0 = chips_gather(up0)
        full_up0 = gat0.reshape(hid, -1)
        norm0 = with_partner(normed(tokens))
        up1 = pair_columns(after(w_up, up0, norm0), 1)
        down0 = chips_gather(w_down[0]).reshape(n_chips * blk, -1)
        full_up1 = chips_gather(up1).reshape(hid, -1)
        down1 = chips_gather(w_down[1]).reshape(n_chips * blk, -1)

        pre0 = dot(norm0, full_up0).astype(jnp.bfloat16)
        kept0, given0 = split(after(gat0, pre0))
        kept0, taken0 = lax.optimization_barrier((kept0, partner(given0)))
        hid0 = gelu_tanh(pre0.astype(jnp.float32)).astype(jnp.bfloat16)
        sums0 = half_sum(hid0, down0, CONTRACT_MID, PIECES)
        step = n_tok // PIECES
        x1 = [(tokens[i * step:(i + 1) * step].astype(jnp.float32) + sums0[i]).astype(jnp.bfloat16) for i in range(PIECES)]
        norms1 = [normed(v) for v in x1]
        norm1 = jnp.concatenate(norms1 + [partner(v) for v in norms1])
        x1 = jnp.concatenate(x1)
        pre1 = dot(norm1, full_up1).astype(jnp.bfloat16)
        hid1 = gelu_tanh(pre1.astype(jnp.float32)).astype(jnp.bfloat16)
        g_pair = with_partner(grad_out)
        g_down1 = chips_scatter(dot(hid1, g_pair, CONTRACT_ROWS))
        d_hid1 = dot(g_pair, down1, CONTRACT_COLS).astype(jnp.bfloat16)
        d_pre1 = gelu_bwd(pre1, d_hid1)
        g_up1 = chips_scatter(dot(norm1, d_pre1, CONTRACT_ROWS))
        dx1 = norm_bwd(x1, grad_out, half_sum(d_pre1, full_up1, CONTRACT_COLS)[0])

        dx1_pair = with_partner(dx1)
        d_hid0 = dot(dx1_pair, down0, CONTRACT_COLS).astype(jnp.bfloat16)
        d_pre0 = gelu_bwd(pre0, d_hid0)
        g_up0 = chips_scatter(dot(norm0, d_pre0, CONTRACT_ROWS))
        g_down0 = chips_scatter(dot(hid0, dx1_pair, CONTRACT_ROWS))
        x_out = (x1.astype(jnp.float32) + half_sum(hid1, down1, CONTRACT_MID)[0]).astype(jnp.bfloat16)
        again0 = partner(taken0)
        full_up0_again = merge(kept0, again0).reshape(hid, -1)
        dx0 = norm_bwd(tokens, dx1, half_sum(d_pre0, full_up0_again, CONTRACT_COLS)[0])

        blocks_up = [row_block(g_up0), row_block(g_up1)]
        grad_up = jnp.stack(blocks_up)
        grad_down = lax.optimization_barrier(jnp.stack([g_down1, g_down1]))
        grad_down = lax.dynamic_update_slice(grad_down, g_down0[None], (0, 0, 0))
        return x_out, dx0, grad_up, grad_down

    return jax.shard_map(device_fn, mesh=mesh3, in_specs=(tok_spec, tok_spec, w_spec, w_spec), out_specs=(tok_spec, tok_spec, w_spec, w_spec), check_vma=False)
```

time: 1830 us -> 1730 us (0.945)
  waiting for transfers between devices: 639 us -> 507 us
  Pallas kernels: 0 us -> 58.7 us
  local copies, waits for them, and re-layouts: 87.1 us -> 59.9 us
    ppermute x4 -> x0, waiting for transfers between devices: 71.1 us -> none  [the longest x1 71.1 us: chips_gather_by_permute(): from_y = lax.ppermute(value, 'y', SWAP)]
    pallas_call x0 -> x6, Pallas kernels: none -> 58.7 us  [the longest x1 18.1 us: split(): pl.pallas_call(kernel, grid=part_grid, out_shape=(part_shape, part_shape)...]
    all_gather x4, waiting for transfers between devices: 265 us -> 206 us  [chips_gather(): return lax.all_gather(value, CHIPS, axis=0, tiled=False)]
    dot_general x16 -> x18, matrix products: 984 us -> 1000 us  [dot(): return lax.dot_general(a, b, dims, preferred_element_type=jnp.float32)]
  transfers between devices with their start and end apart: 24 -> 24, of which waited for: 11 -> 10; matrix products, arithmetic and copies ran while one was open for 48% -> 52% of each run, Pallas kernels for 0% -> 3%
where the time goes in v2:
time: 1730 us
  matrix products  1000 us (58%)
  waiting for transfers between devices  507 us (29%)
  other arithmetic  79.2 us (5%)
  local copies, waits for them, and re-layouts  59.9 us (3%)
  Pallas kernels  58.7 us (3%)
    dot_general x18, matrix products, dot(): return lax.dot_general(a, b, dims, preferred_element_type=jnp.float32)  1000 us
    reduce_scatter x4, waiting for transfers between devices, chips_scatter(): return lax.psum_scatter(value, CHIPS, scatter_dimension=0, tiled=True)  270 us
    all_gather x4, waiting for transfers between devices, chips_gather(): return lax.all_gather(value, CHIPS, axis=0, tiled=False)  206 us
  transfers between devices with their start and end apart: 24, of which 10 were waited for; matrix products, arithmetic and copies ran while one was open for 52% of the time, Pallas kernels for 3%

profile of v2, /device:TPU:0, one launch (start us, length us, event | category | flops | bytes accessed | tf_op | source)
XLA Modules:
  0.0 1726.4 jit_solution(9250124704625076273)
XLA Ops:
  7.2 5.9 pick.2
  13.1 0.8 collective-permute-start.1
  13.9 3.5 collective-permute-done.1.other_ref
  17.4 1.2 copy-done.8
  18.5 5.4 join.2
  24.0 6.4 fusion.77
  30.4 5.4 fusion.38
  35.8 0.6 copy-done.10
  36.4 0.6 copy-done.12
  37.0 6.9 fusion.39
  44.3 5.9 pick.3
  50.4 6.4 collective-permute-done.6.other_ref
  56.8 1.2 copy-done.9
  58.0 5.4 join.3
  63.7 89.4 %all-gather.11.cloned.1.call-done = bf16[8,192,4480]{2,1,0:T(8,128)(2,1)} async-done(((bf16[2,192,4480]{2,1,0:T(8,128)(2,1)}), bf16[8,192,4480]{2,1,0:T(8,128)(2,1)}) %all-gather.11.cloned.1.call-update) | async-done | bytes 13762576 | tf_op jit(solution)/shard_map/all_gather | solution.py:142
  153.1 80.9 %fusion.13 = (bf16[4096,4480]{1,0:T(8,128)(2,1)}, bf16[4096,4480]{1,0:T(8,128)(2,1)}) fusion(bf16[1536,4480]{1,0:T(8,128)(2,1)} %bitcast.41, bf16[2048,1536]{1,0:T(8,128)(2,1)} %collective-permute-done, bf16[2048,1536]{1,0:T(8,128)(2,1)} %fusion.39), kind=kOutput, calls=%fused_computation.25 | convolution fusion | flops 56598462464 | bytes 99745792 | tf_op jit(solution)/shard_map/dot_general | solution.py:27
  234.0 48.1 %all-gather.7.cloned.1.call-done = bf16[4,1120,1536]{2,1,0:T(8,128)(2,1)} async-done(((bf16[1,1120,1536]{2,1,0:T(8,128)(2,1)}), bf16[4,1120,1536]{2,1,0:T(8,128)(2,1)}) %all-gather.7.cloned.1.call-update) | async-done | bytes 13762576 | tf_op jit(solution)/shard_map/all_gather | solution.py:142
  282.1 18.9 %fusion.56 = f32[1024,1536]{1,0:T(8,128)S(1)} fusion(bf16[4480,1536]{1,0:T(8,128)(2,1)} %bitcast.46, bf16[4096,4480]{1,0:T(8,128)(2,1)} %get-tuple-element.50), kind=kOutput, calls=%fused_computation.81 | convolution fusion | flops 14092861440 | bytes 29229056 | tf_op jit(solution)/shard_map/dot_general | solution.py:27
  301.1 21.8 %fusion.52 = f32[1024,1536]{1,0:T(8,128)} fusion(bf16[4480,1536]{1,0:T(8,128)(2,1)} %bitcast.47, bf16[4096,4480]{1,0:T(8,128)(2,1)} %get-tuple-element.50), kind=kOutput, calls=%fused_computation.77 | convolution fusion | flops 14092861440 | bytes 29229056 | tf_op jit(solution)/shard_map/dot_general | solution.py:27
  323.3 20.8 %fusion.61 = (f32[1024]{0:T(1024)S(1)}, bf16[1024,1536]{1,0:T(8,128)(2,1)S(1)}) fusion(f32[1024,1536]{1,0:T(8,128)S(1)} %collective-permute-done.2, bf16[4480,1536]{1,0:T(8,128)(2,1)} %bitcast.48, bf16[4096,4480]{1,0:T(8,128)(2,1)} %get-tuple-element.50, bf16[2048,1536]{1,0:T(8,128)(2,1)S(1)} %bitcast.38), kind=kOutput, calls=%fused_computation.91 | convolution fusion | flops 14103870464 | bytes 35524608 | tf_op jit(solution)/shard_map/dot_general | solution.py:27
  344.2 0.6 fusion.62
  345.1 22.5 %fusion.63 = (f32[1024]{0:T(1024)S(1)}, bf16[1024,1536]{1,0:T(8,128)(2,1)S(1)}) fusion(f32[1024,1536]{1,0:T(8,128)} %collective-permute-done.3, bf16[4480,1536]{1,0:T(8,128)(2,1)} %bitcast.49, bf16[4096,4480]{1,0:T(8,128)(2,1)} %get-tuple-element.50, bf16[2048,1536]{1,0:T(8,128)(2,1)S(1)} %bitcast.38), kind=kOutput, calls=%fused_computation.93 | convolution fusion | flops 14103870464 | bytes 35524608 | tf_op jit(solution)/shard_map/dot_general | solution.py:27
  367.7 1.6 copy-done.5
  369.3 2.2 fusion.64
  372.0 5.9 constant_dynamic-update-slice_fusion.1
  377.9 5.9 constant_dynamic-update-slice_fusion
  383.8 26.7 %all-gather.13.cloned.1.call-done = bf16[8,192,4480]{2,1,0:T(8,128)(2,1)} async-done(((bf16[2,192,4480]{2,1,0:T(8,128)(2,1)}), bf16[8,192,4480]{2,1,0:T(8,128)(2,1)}) %all-gather.13.cloned.1.call-update) | async-done | bytes 13762576 | tf_op jit(solution)/shard_map/all_gather | solution.py:142
  410.6 87.0 %fusion.19 = (bf16[4096,4480]{1,0:T(8,128)(2,1)}, bf16[4096,4480]{1,0:T(8,128)(2,1)}) fusion(bf16[1536,4480]{1,0:T(8,128)(2,1)} %bitcast.54, bf16[1024,1536]{1,0:T(8,128)(2,1)} %collective-permute-done.5, bf16[1024,1536]{1,0:T(8,128)(2,1)} %collective-permute-done.4, bf16[1024,1536]{1,0:T(8,128)(2,1)} %fusion.64, bf16[1024,1536]{1,0:T(8,128)(2,1)S(1)} %fusion.62), kind=kOutput, calls=%fused_computation.31 | convolution fusion | flops 56623628288 | bytes 99745792 | tf_op jit(solution)/shard_map/dot_general | solution.py:27
  497.5 41.9 %all-gather.9.cloned.1.call-done = bf16[4,1120,1536]{2,1,0:T(8,128)(2,1)} async-done(((bf16[1,1120,1536]{2,1,0:T(8,128)(2,1)}), bf16[4,1120,1536]{2,1,0:T(8,128)(2,1)}) %all-gather.9.cloned.1.call-update) | async-done | bytes 13762576 | tf_op jit(solution)/shard_map/all_gather | solution.py:142
  539.5 115.1 %fusion.4 = bf16[4096,4480]{1,0:T(8,128)(2,1)} fusion(bf16[4096,4480]{1,0:T(8,128)(2,1)} %get-tuple-element.57, bf16[4096,1536]{1,0:T(8,128)(2,1)} %constant_dynamic-update-slice_fusion, bf16[4480,1536]{1,0:T(8,128)(2,1)} %bitcast.51), kind=kOutput, calls=%fused_computation.16 | convolution fusion | flops 56793497600 | bytes 99745792 | tf_op jit(solution)/shard_map/dot_general | solution.py:27
  654.6 81.3 %fusion.69 = f32[1536,4480]{1,0:T(8,128)} fusion(bf16[4096,4480]{1,0:T(8,128)(2,1)} %fusion.4, bf16[1024,1536]{1,0:T(8,128)(2,1)} %collective-permute-done.5, bf16[1024,1536]{1,0:T(8,128)(2,1)} %collective-permute-done.4, bf16[1024,1536]{1,0:T(8,128)(2,1)} %fusion.64, bf16[1024,1536]{1,0:T(8,128)(2,1)S(1)} %copy-done.7), kind=kOutput, calls=%fused_computation.102 | convolution fusion | flops 56421777408 | bytes 76808192 | tf_op jit(solution)/shard_map/dot_general | solution.py:27
  736.0 39.1 %fusion.26 = f32[2048,1536]{1,0:T(8,128)} fusion(bf16[1536,4480]{1,0:T(8,128)(2,1)} %bitcast.55, bf16[4096,4480]{1,0:T(8,128)(2,1)} %fusion.4), kind=kOutput, calls=%fused_computation.52 | convolution fusion | flops 28185722880 | bytes 44695552 | tf_op jit(solution)/shard_map/dot_general | solution.py:27
  775.1 68.5 %fusion.82 = f32[4480,1536]{1,0:T(8,128)} fusion(bf16[4096,4480]{1,0:T(8,128)(2,1)} %get-tuple-element.56, bf16[4096,1536]{1,0:T(8,128)(2,1)} %constant_dynamic-update-slice_fusion), kind=kOutput, calls=%fused_computation.127 | convolution fusion | flops 56371445760 | bytes 76808192 | tf_op jit(solution)/shard_map/dot_general | solution.py:27
  843.7 1.9 copy-done.3
  845.6 39.6 %fusion.42 = (f32[2048]{0:T(1024)S(1)}, f32[2048]{0:T(1024)S(1)}, f32[2048,1536]{1,0:T(8,128)}) fusion(bf16[1024,1536]{1,0:T(8,128)(2,1)} %copy-done.5, bf16[1024,1536]{1,0:T(8,128)(2,1)S(1)} %copy-done.3, f32[2048,1536]{1,0:T(8,128)} %collective-permute-done.9, bf16[1536,4480]{1,0:T(8,128)(2,1)} %bitcast.56, bf16[4096,4480]{1,0:T(8,128)(2,1)} %fusion.4), kind=kOutput, calls=%fused_computation.70 | convolution fusion | flops 28214030336 | bytes 63586304 | tf_op jit(solution)/shard_map/dot_general | solution.py:27
  885.2 10.1 fusion.35
  895.3 2.7 copy-done.1
  898.2 9.9 collective-permute-done.10
  908.1 2.7 copy-done.14
  910.8 110.6 %fusion.7 = bf16[4096,4480]{1,0:T(8,128)(2,1)} fusion(bf16[4096,4480]{1,0:T(8,128)(2,1)} %get-tuple-element.51, bf16[4480,1536]{1,0:T(8,128)(2,1)} %bitcast.50, bf16[2048,1536]{1,0:T(8,128)(2,1)} %copy-done.14, bf16[2048,1536]{1,0:T(8,128)(2,1)} %copy-done.1), kind=kOutput, calls=%fused_computation.19 | convolution fusion | flops 56818663424 | bytes 99745792 | tf_op jit(solution)/shard_map/dot_general | solution.py:27
  1021.5 71.4 %fusion.76 = f32[1536,4480]{1,0:T(8,128)} fusion(bf16[4096,4480]{1,0:T(8,128)(2,1)} %fusion.7, bf16[2048,1536]{1,0:T(8,128)(2,1)} %collective-permute-done, bf16[2048,1536]{1,0:T(8,128)(2,1)} %fusion.39), kind=kOutput, calls=%fused_computation.121 | convolution fusion | flops 56396611584 | bytes 76808192 | tf_op jit(solution)/shard_map/dot_general | solution.py:27
  1092.9 68.2 %fusion.60 = f32[4480,1536]{1,0:T(8,128)} fusion(bf16[4096,4480]{1,0:T(8,128)(2,1)} %get-tuple-element.50, bf16[2048,1536]{1,0:T(8,128)(2,1)} %copy-done.14, bf16[2048,1536]{1,0:T(8,128)(2,1)} %copy-done.1), kind=kOutput, calls=%fused_computation.85 | convolution fusion | flops 56396611584 | bytes 76808192 | tf_op jit(solution)/shard_map/dot_general | solution.py:27
  1161.2 18.1 %split.1 = (bf16[4,192,4480]{2,1,0:T(8,128)(2,1)}, bf16[4,192,4480]{2,1,0:T(8,128)(2,1)}) custom-call(bf16[4,2,192,4480]{3,2,1,0:T(8,128)(2,1)} %bitcast.42), custom_call_target="tpu_custom_call" | custom-call | tf_op jit(solution)/shard_map/split/pallas_call | solution.py:122
  1179.7 10.8 collective-permute-done.11
  1190.9 38.3 %fusion.30 = f32[2048,1536]{1,0:T(8,128)} fusion(bf16[4480,1536]{1,0:T(8,128)(2,1)} %bitcast.52, bf16[4096,4480]{1,0:T(8,128)(2,1)} %get-tuple-element.56), kind=kOutput, calls=%fused_computation.56 | convolution fusion | flops 28185722880 | bytes 44695552 | tf_op jit(solution)/shard_map/dot_general | solution.py:27
  1229.2 18.0 %merge.1 = bf16[4,2,192,4480]{3,2,1,0:T(8,128)(2,1)} custom-call(bf16[4,192,4480]{2,1,0:T(8,128)(2,1)} %get-tuple-element.22.keep_ref, bf16[4,192,4480]{2,1,0:T(8,128)(2,1)} %collective-permute-done.12.take_ref), custom_call_target="tpu_custom_call" | custom-call | tf_op jit(solution)/shard_map/merge/pallas_call | solution.py:139
  1247.2 38.9 %fusion.22 = f32[2048,1536]{1,0:T(8,128)} fusion(bf16[1536,4480]{1,0:T(8,128)(2,1)} %bitcast.43, bf16[4096,4480]{1,0:T(8,128)(2,1)} %fusion.7), kind=kOutput, calls=%fused_computation.48 | convolution fusion | flops 28185722880 | bytes 44695552 | tf_op jit(solution)/shard_map/dot_general | solution.py:27
  1286.2 39.5 %fusion.41 = bf16[2048,1536]{1,0:T(8,128)(2,1)} fusion(f32[2048,1536]{1,0:T(8,128)} %collective-permute-done.7, bf16[4480,1536]{1,0:T(8,128)(2,1)} %bitcast.53, bf16[4096,4480]{1,0:T(8,128)(2,1)} %get-tuple-element.56, bf16[1024,1536]{1,0:T(8,128)(2,1)} %copy-done.5, bf16[1024,1536]{1,0:T(8,128)(2,1)S(1)} %copy-done.4), kind=kOutput, calls=%fused_computation.69 | convolution fusion | flops 28207742976 | bytes 57278464 | tf_op jit(solution)/shard_map/dot_general | solution.py:27
  1325.7 40.1 %fusion.40 = (f32[2048]{0:T(1024)S(1)}, f32[2048,1536]{1,0:T(8,128)}) fusion(bf16[2048,1536]{1,0:T(8,128)(2,1)} %param.4, f32[2048,1536]{1,0:T(8,128)} %collective-permute-done.13, bf16[1536,4480]{1,0:T(8,128)(2,1)} %bitcast.44, bf16[4096,4480]{1,0:T(8,128)(2,1)} %fusion.7), kind=kOutput, calls=%fused_computation.68 | convolution fusion | flops 28198303744 | bytes 63578112 | tf_op jit(solution)/shard_map/dot_general | solution.py:27
  1365.8 5.6 slice_select_fusion
  1371.4 0.5 collective-permute-start.15
  1372.1 11.2 fusion.37
  1383.3 11.7 pad_maximum_fusion.1
  1395.0 52.9 %reduce-scatter.5.cloned.1.call-done = f32[384,4480]{1,0:T(8,128)} async-done(((f32[1536,4480]{1,0:T(8,128)}), f32[384,4480]{1,0:T(8,128)}) %reduce-scatter.5.cloned.1.call-update) | async-done | bytes 6881296 | tf_op jit(solution)/shard_map/reduce_scatter | solution.py:145
  1447.9 5.1 slice_select_fusion.2
  1453.1 4.8 broadcast_select_fusion
  1457.8 3.2 fusion.80
  1461.0 8.3 concatenate.27
  1469.3 216.9 %reduce-scatter.11.cloned.1.call-done = f32[1120,1536]{1,0:T(8,128)} async-done(((f32[4480,1536]{1,0:T(8,128)}), f32[1120,1536]{1,0:T(8,128)}) %reduce-scatter.11.cloned.1.call-update) | async-done | bytes 6881296 | tf_op jit(solution)/shard_map/reduce_scatter | solution.py:145
  1686.2 6.4 bitcast_dynamic-update-slice_fusion
  1692.6 4.6 broadcast_select_fusion.2
  1697.2 3.2 fusion.78
  1700.4 8.0 concatenate.26
  1708.4 11.0 pad_maximum_fusion
  (76 shorter events, 3.8 us)
Async XLA Ops:
  7.2 145.9 %all-gather.11.cloned.1.call-start = ((), (), s32[]{:S(2)}) async-start(), calls=%async_computation.10 | async-start | bytes 17203200 | tf_op jit(solution)/shard_map/all_gather | solution.py:142
  13.1 4.3 collective-permute-start.1
  17.4 1.2 copy-start.8
  23.9 258.2 %all-gather.7.cloned.1.call-start = ((), (), s32[]{:S(2)}) async-start(), calls=%async_computation.4 | async-start | bytes 17203200 | tf_op jit(solution)/shard_map/all_gather | solution.py:142
  30.4 380.2 %all-gather.13.cloned.1.call-start = ((), (), s32[]{:S(2)}) async-start(), calls=%async_computation.11 | async-start | bytes 17203200 | tf_op jit(solution)/shard_map/all_gather | solution.py:142
  35.8 0.6 copy-start.10
  36.4 0.6 copy-start.12
  44.0 19.7 %collective-permute-start = (bf16[2048,1536]{1,0:T(8,128)(2,1)}, bf16[2048,1536]{1,0:T(8,128)(2,1)}, u32[]{:S(2)}, u32[]{:S(2)}) collective-permute-start(bf16[2048,1536]{1,0:T(8,128)(2,1)} %fusion.39), channel_id=1, source_target_pairs={{0,1},{1,0},{2,3},{3,2},{4,5},{5,4},{6,7},{7,6}} | collective-permute-start | bytes 18874376 | tf_op jit(solution)/shard_map/ppermute | solution.py:31
  50.2 6.5 collective-permute-start.6
  56.8 1.2 copy-start.9
  63.4 476.0 %all-gather.9.cloned.1.call-start = ((), (), s32[]{:S(2)}) async-start(), calls=%async_computation.5 | async-start | bytes 17203200 | tf_op jit(solution)/shard_map/all_gather | solution.py:142
  282.1 41.2 %slice-start = ((s8[6291456]{0:T(1024)(128)(4,1)}), s8[4194304]{0:T(1024)(128)(4,1)S(1)}, s32[]{:S(2)}) async-start(s8[6291456]{0:T(1024)(128)(4,1)} %bitcast.37), calls=%async_computation.12 | async-start | bytes 8388608
  301.0 22.3 %slice-start.1 = ((s8[6291456]{0:T(1024)(128)(4,1)}), s8[2097152]{0:T(1024)(128)(4,1)S(1)}, s32[]{:S(2)}) async-start(s8[6291456]{0:T(1024)(128)(4,1)} %bitcast.37), calls=%async_computation.13 | async-start | bytes 4194304
  301.0 22.3 %collective-permute-start.2 = (f32[1024,1536]{1,0:T(8,128)S(1)}, f32[1024,1536]{1,0:T(8,128)S(1)}, u32[]{:S(2)}, u32[]{:S(2)}) collective-permute-start(f32[1024,1536]{1,0:T(8,128)S(1)} %fusion.56), channel_id=1, source_target_pairs={{0,1},{1,0},{2,3},{3,2},{4,5},{5,4},{6,7},{7,6}} | collective-permute-start | bytes 18874376 | tf_op jit(solution)/shard_map/ppermute | solution.py:31
  322.8 22.3 %collective-permute-start.3 = (f32[1024,1536]{1,0:T(8,128)}, f32[1024,1536]{1,0:T(8,128)}, u32[]{:S(2)}, u32[]{:S(2)}) collective-permute-start(f32[1024,1536]{1,0:T(8,128)} %fusion.52), channel_id=1, source_target_pairs={{0,1},{1,0},{2,3},{3,2},{4,5},{5,4},{6,7},{7,6}} | collective-permute-start | bytes 18874376 | tf_op jit(solution)/shard_map/ppermute | solution.py:31
  323.2 54.8 %collective-permute-start.8 = (bf16[2048,1536]{1,0:T(8,128)(2,1)}, bf16[2048,1536]{1,0:T(8,128)(2,1)}, u32[]{:S(2)}, u32[]{:S(2)}) collective-permute-start(bf16[2048,1536]{1,0:T(8,128)(2,1)} %param.5), channel_id=1, source_target_pairs={{0,1},{1,0},{2,3},{3,2},{4,5},{5,4},{6,7},{7,6}} | collective-permute-start | bytes 18874376 | tf_op jit(solution)/shard_map/ppermute | solution.py:31
  344.2 23.5 %copy-start.2 = (bf16[1024,1536]{1,0:T(8,128)(2,1)}, bf16[1024,1536]{1,0:T(8,128)(2,1)S(1)}, u32[]{:S(2)}) copy-start(bf16[1024,1536]{1,0:T(8,128)(2,1)S(1)} %get-tuple-element.55) | copy-start | bytes 9437188
  344.8 65.8 %copy-start.6 = (bf16[1024,1536]{1,0:T(8,128)(2,1)}, bf16[1024,1536]{1,0:T(8,128)(2,1)S(1)}, u32[]{:S(2)}) copy-start(bf16[1024,1536]{1,0:T(8,128)(2,1)S(1)} %fusion.62) | copy-start | bytes 9437188
  344.8 65.8 %collective-permute-start.4 = (bf16[1024,1536]{1,0:T(8,128)(2,1)S(1)}, bf16[1024,1536]{1,0:T(8,128)(2,1)}, u32[]{:S(2)}, u32[]{:S(2)}) collective-permute-start(bf16[1024,1536]{1,0:T(8,128)(2,1)S(1)} %fusion.62), channel_id=1, source_target_pairs={{0,1},{1,0},{2,3},{3,2},{4,5},{5,4},{6,7},{7,6}} | collective-permute-start | bytes 9437192 | tf_op jit(solution)/shard_map/ppermute | solution.py:31
  367.7 1.6 copy-start.5
  371.6 39.0 %collective-permute-start.5 = (bf16[1024,1536]{1,0:T(8,128)(2,1)}, bf16[1024,1536]{1,0:T(8,128)(2,1)}, u32[]{:S(2)}, u32[]{:S(2)}) collective-permute-start(bf16[1024,1536]{1,0:T(8,128)(2,1)} %fusion.64), channel_id=1, source_target_pairs={{0,1},{1,0},{2,3},{3,2},{4,5},{5,4},{6,7},{7,6}} | collective-permute-start | bytes 9437192 | tf_op jit(solution)/shard_map/ppermute | solution.py:31
  372.0 993.8 %reduce-scatter.7.cloned.1.call-start = ((), (), s32[]{:S(2)}) async-start(), calls=%async_computation.7 | async-start | bytes 34406400 | tf_op jit(solution)/shard_map/reduce_scatter | solution.py:145
  539.4 115.1 %copy-start.7 = (bf16[1024,1536]{1,0:T(8,128)(2,1)S(1)}, bf16[1024,1536]{1,0:T(8,128)(2,1)}, u32[]{:S(2)}) copy-start(bf16[1024,1536]{1,0:T(8,128)(2,1)} %copy-done.6) | copy-start | bytes 9437188
  735.9 647.3 %reduce-scatter.9.cloned.1.call-start = ((), (), s32[]{:S(2)}) async-start(), calls=%async_computation.8 | async-start | bytes 34406400 | tf_op jit(solution)/shard_map/reduce_scatter | solution.py:145
  775.1 68.6 %collective-permute-start.9 = (f32[2048,1536]{1,0:T(8,128)}, f32[2048,1536]{1,0:T(8,128)}, u32[]{:S(2)}, u32[]{:S(2)}) collective-permute-start(f32[2048,1536]{1,0:T(8,128)} %fusion.26), channel_id=1, source_target_pairs={{0,1},{1,0},{2,3},{3,2},{4,5},{5,4},{6,7},{7,6}} | collective-permute-start | bytes 37748744 | tf_op jit(solution)/shard_map/ppermute | solution.py:31
  843.6 2.0 copy-start.3
  843.6 604.3 %reduce-scatter.5.cloned.1.call-start = ((), (), s32[]{:S(2)}) async-start(), calls=%async_computation.6 | async-start | bytes 34406400 | tf_op jit(solution)/shard_map/reduce_scatter | solution.py:145
  895.3 2.7 copy-start.1
  898.0 10.2 collective-permute-start.10
  908.1 2.7 copy-start.14
  1092.9 593.4 %reduce-scatter.11.cloned.1.call-start = ((), (), s32[]{:S(2)}) async-start(), calls=%async_computation.9 | async-start | bytes 34406400 | tf_op jit(solution)/shard_map/reduce_scatter | solution.py:145
  1179.3 11.2 collective-permute-start.11
  1190.5 38.6 %collective-permute-start.12 = (bf16[4,192,4480]{2,1,0:T(8,128)(2,1)S(1)}, bf16[4,192,4480]{2,1,0:T(8,128)(2,1)}, u32[]{:S(2)}, u32[]{:S(2)}) collective-permute-start(bf16[4,192,4480]{2,1,0:T(8,128)(2,1)S(1)} %collective-permute-done.11), channel_id=1, source_target_pairs={{0,1},{1,0},{2,3},{3,2},{4,5},{5,4},{6,7},{7,6}} | collective-permute-start | bytes 20643848 | tf_op jit(solution)/shard_map/ppermute | solution.py:31
  1229.2 57.0 %collective-permute-start.7 = (f32[2048,1536]{1,0:T(8,128)}, f32[2048,1536]{1,0:T(8,128)}, u32[]{:S(2)}, u32[]{:S(2)}) collective-permute-start(f32[2048,1536]{1,0:T(8,128)} %fusion.30), channel_id=1, source_target_pairs={{0,1},{1,0},{2,3},{3,2},{4,5},{5,4},{6,7},{7,6}} | collective-permute-start | bytes 37748744 | tf_op jit(solution)/shard_map/ppermute | solution.py:31
  1247.2 39.0 %copy-start.4 = (bf16[1024,1536]{1,0:T(8,128)(2,1)S(1)}, bf16[1024,1536]{1,0:T(8,128)(2,1)}, u32[]{:S(2)}) copy-start(bf16[1024,1536]{1,0:T(8,128)(2,1)} %copy-done.2) | copy-start | bytes 9437188
  1286.1 39.6 %collective-permute-start.13 = (f32[2048,1536]{1,0:T(8,128)}, f32[2048,1536]{1,0:T(8,128)}, u32[]{:S(2)}, u32[]{:S(2)}) collective-permute-start(f32[2048,1536]{1,0:T(8,128)} %fusion.22), channel_id=1, source_target_pairs={{0,1},{1,0},{2,3},{3,2},{4,5},{5,4},{6,7},{7,6}} | collective-permute-start | bytes 37748744 | tf_op jit(solution)/shard_map/ppermute | solution.py:31
  1325.7 40.1 %copy-start.11 = (f32[2048]{0:T(1024)S(1)}, f32[2048]{0:T(1024)}, u32[]{:S(2)}) copy-start(f32[2048]{0:T(1024)} %copy-done.10) | copy-start | bytes 24580
  1325.7 46.2 %copy-start.13 = (f32[2048]{0:T(1024)S(1)}, f32[2048]{0:T(1024)}, u32[]{:S(2)}) copy-start(f32[2048]{0:T(1024)} %copy-done.12) | copy-start | bytes 24580
  1365.8 6.3 copy-start
  1371.4 81.7 %collective-permute-start.15 = (f32[192,4480]{1,0:T(8,128)}, f32[192,4480]{1,0:T(8,128)S(1)}, u32[]{:S(2)}, u32[]{:S(2)}) collective-permute-start(f32[192,4480]{1,0:T(8,128)} %slice_select_fusion), channel_id=1, source_target_pairs={{0,1},{1,0},{2,3},{3,2},{4,5},{5,4},{6,7},{7,6}} | collective-permute-start | bytes 10321928 | tf_op jit(solution)/shard_map/ppermute | solution.py:31
  1453.0 239.6 %collective-permute-start.14 = (f32[192,4480]{1,0:T(8,128)}, f32[192,4480]{1,0:T(8,128)}, u32[]{:S(2)}, u32[]{:S(2)}) collective-permute-start(f32[192,4480]{1,0:T(8,128)} %slice_select_fusion.2), channel_id=1, source_target_pairs={{0,1},{1,0},{2,3},{3,2},{4,5},{5,4},{6,7},{7,6}} | collective-permute-start | bytes 10321928 | tf_op jit(solution)/shard_map/ppermute | solution.py:31
Sparse Core Ops, SparseCore 0:
  24.1 128.9 all-gather.10
  155.4 126.6 all-gather.6
  283.9 126.6 all-gather.12
  412.8 126.6 all-gather.8
  736.1 235.2 reduce-scatter.6
  974.2 235.2 reduce-scatter.8
  1212.6 235.2 reduce-scatter.4
  1450.9 235.2 reduce-scatter.10

commit v3 on v2

--- a/solution.py
+++ b/solution.py
@@ -35,10 +35,6 @@
     return jnp.concatenate([value, partner(value)], axis=0)
 
 
-def after(value, *others):
-    return lax.optimization_barrier((value, *others))[0]
-
-
 def solution(mesh):
     n_y = mesh.shape['local']
     n_x = mesh.shape['data'] // 2
@@ -53,29 +49,29 @@
         blk = w_down.shape[1]
         n_tok = tokens.shape[0]
 
-        def pick(layer):
+        def pick(whole, first_index, count):
             def kernel(w_ref, mine_ref, other_ref):
                 is_even = lax.axis_index('core') == 0
 
-                def copy(first, mine, other):
+                def copy(first):
                     for k in range(n_chips):
                         dst = slice(k * blk, (k + 1) * blk)
-                        mine[:, dst] = w_ref[:, (2 * k + first) * blk:(2 * k + first + 1) * blk]
-                        other[:, dst] = w_ref[:, (2 * k + 1 - first) * blk:(2 * k + 2 - first) * blk]
+                        mine_ref[:, dst] = w_ref[:, (2 * k + first) * blk:(2 * k + first + 1) * blk]
+                        other_ref[:, dst] = w_ref[:, (2 * k + 1 - first) * blk:(2 * k + 2 - first) * blk]
 
                 @pl.when(is_even)
                 def _():
-                    copy(0, mine_ref, other_ref)
+                    copy(0)
 
                 @pl.when(jnp.logical_not(is_even))
                 def _():
-                    copy(1, mine_ref, other_ref)
+                    copy(1)
 
-            half = jax.ShapeDtypeStruct((rows, ffn // 2), w_up.dtype)
-            spec = pl.BlockSpec((ROW_TILE, ffn // 2), lambda i: (i, 0))
+            half = jax.ShapeDtypeStruct((count, rows, ffn // 2), w_up.dtype)
+            spec = pl.BlockSpec((None, ROW_TILE, ffn // 2), lambda c, i: (c, i, 0))
             return pl.pallas_call(
-                kernel, grid=(rows // ROW_TILE,), out_shape=(half, half),
-                in_specs=[pl.BlockSpec((None, ROW_TILE, ffn), lambda i: (layer, i, 0))], out_specs=(spec, spec), name='pick')
+                kernel, grid=(count, rows // ROW_TILE), out_shape=(half, half),
+                in_specs=[pl.BlockSpec((None, ROW_TILE, ffn), lambda c, i: (c + first_index, i, 0))], out_specs=(spec, spec), name='pick')(whole)
 
         def join(mine, other):
             def kernel(mine_ref, other_ref, out_ref):
@@ -97,29 +93,12 @@
                 in_specs=[spec, spec], out_specs=pl.BlockSpec((2, ROW_TILE, ffn // 2), lambda i: (0, i, 0)), name='join')(mine, other)
 
         def pair_columns(w, layer):
-            mine, other = pick(layer)(w)
-            return join(mine, partner(other))
+            mine, other = pick(w, layer, 1)
+            return join(mine[0], partner(other[0]))
 
         whole_spec = pl.BlockSpec((1, 2, ROW_TILE, ffn // 2), lambda c, i: (c, 0, i, 0))
         part_spec = pl.BlockSpec((1, ROW_TILE, ffn // 2), lambda c, i: (c, i, 0))
-        part_shape = jax.ShapeDtypeStruct((n_chips, rows, ffn // 2), w_up.dtype)
         part_grid = (n_chips, rows // ROW_TILE)
-
-        def split(whole):
-            def kernel(whole_ref, keep_ref, give_ref):
-                is_even = lax.axis_index('core') == 0
-
-                @pl.when(is_even)
-                def _():
-                    keep_ref[...] = whole_ref[:, 0]
-                    give_ref[...] = whole_ref[:, 1]
-
-                @pl.when(jnp.logical_not(is_even))
-                def _():
-                    keep_ref[...] = whole_ref[:, 1]
-                    give_ref[...] = whole_ref[:, 0]
-
-            return pl.pallas_call(kernel, grid=part_grid, out_shape=(part_shape, part_shape), in_specs=[whole_spec], out_specs=(part_spec, part_spec), name='split')(whole)
 
         def merge(kept, taken):
             def kernel(keep_ref, take_ref, whole_ref):
@@ -170,19 +149,17 @@
         def normed(x):
             return rms_norm(x.astype(jnp.float32)).astype(jnp.bfloat16)
 
-        up0 = pair_columns(w_up, 0)
         hid = n_chips * 2 * rows
-        gat0 = chips_gather(up0)
-        full_up0 = gat0.reshape(hid, -1)
+        mine0, other0 = pick(chips_gather(w_up[0]), 0, n_chips)
+        full_up0 = merge(mine0, partner(other0)).reshape(hid, -1)
         norm0 = with_partner(normed(tokens))
-        up1 = pair_columns(after(w_up, up0, norm0), 1)
+        up1 = pair_columns(w_up, 1)
         down0 = chips_gather(w_down[0]).reshape(n_chips * blk, -1)
         full_up1 = chips_gather(up1).reshape(hid, -1)
         down1 = chips_gather(w_down[1]).reshape(n_chips * blk, -1)
 
         pre0 = dot(norm0, full_up0).astype(jnp.bfloat16)
-        kept0, given0 = split(after(gat0, pre0))
-        kept0, taken0 = lax.optimization_barrier((kept0, partner(given0)))
+        mine0, other0 = lax.optimization_barrier((mine0, other0, pre0))[:2]
         hid0 = gelu_tanh(pre0.astype(jnp.float32)).astype(jnp.bfloat16)
         sums0 = half_sum(hid0, down0, CONTRACT_MID, PIECES)
         step = n_tok // PIECES
@@ -205,8 +182,8 @@
         g_up0 = chips_scatter(dot(norm0, d_pre0, CONTRACT_ROWS))
         g_down0 = chips_scatter(dot(hid0, dx1_pair, CONTRACT_ROWS))
         x_out = (x1.astype(jnp.float32) + half_sum(hid1, down1, CONTRACT_MID)[0]).astype(jnp.bfloat16)
-        again0 = partner(taken0)
-        full_up0_again = merge(kept0, again0).reshape(hid, -1)
+        again0 = partner(other0)
+        full_up0_again = merge(mine0, again0).reshape(hid, -1)
         dx0 = norm_bwd(tokens, dx1, half_sum(d_pre0, full_up0_again, CONTRACT_COLS)[0])
 
         blocks_up = [row_block(g_up0), row_block(g_up1)]

time: 1730 us -> 1720 us (level)
  waiting for transfers between devices: 507 us -> 484 us
    all_gather x4, waiting for transfers between devices: 206 us -> 166 us  [chips_gather(): return lax.all_gather(value, CHIPS, axis=0, tiled=False)]
    reduce_scatter x4, waiting for transfers between devices: 270 us -> 298 us  [chips_scatter(): return lax.psum_scatter(value, CHIPS, scatter_dimension=0, tiled=True)]
    pallas_call x1 -> x2, Pallas kernels: 18 us -> 35.8 us  [merge(): pl.pallas_call(kernel, grid=part_grid, out_shape=shape, in_specs=[part_sp...]
  transfers between devices with their start and end apart: 24 -> 23, of which waited for: 10 -> 7; matrix products, arithmetic and copies ran while one was open for 52% -> 53% of each run, Pallas kernels for 3% -> 4%
where the time goes in v3:
time: 1720 us; the launch traced here: 1710 us
  matrix products  1000 us (58%)
  waiting for transfers between devices  484 us (28%)
  other arithmetic  79.1 us (5%)
  Pallas kernels  67.3 us (4%)
  local copies, waits for them, and re-layouts  62.7 us (4%)
    dot_general x18, matrix products, dot(): return lax.dot_general(a, b, dims, preferred_element_type=jnp.float32)  1000 us
    reduce_scatter x4, waiting for transfers between devices, chips_scatter(): return lax.psum_scatter(value, CHIPS, scatter_dimension=0, tiled=True)  298 us
    all_gather x4, waiting for transfers between devices, chips_gather(): return lax.all_gather(value, CHIPS, axis=0, tiled=False)  166 us
    pallas_call x2, Pallas kernels, merge(): pl.pallas_call(kernel, grid=part_grid, out_shape=shape, in_specs=[part_sp...  35.8 us
  transfers between devices with their start and end apart: 23, of which 7 were waited for; matrix products, arithmetic and copies ran while one was open for 53% of the time, Pallas kernels for 4%

profile of v3, /device:TPU:0, one launch (start us, length us, event | category | flops | bytes accessed | tf_op | source)
XLA Modules:
  0.0 1714.2 jit_solution(7854667632295781844)
XLA Ops:
  7.2 4.0 slice.110
  11.2 6.4 fusion.79
  17.7 5.5 fusion.38
  23.2 0.6 copy-done.9
  23.8 117.0 %all-gather.6.cloned.1.call-done.w_ref = bf16[4,192,8960]{2,1,0:T(8,128)(2,1)} async-done(((bf16[1,192,8960]{2,1,0:T(8,128)(2,1)}), bf16[4,192,8960]{2,1,0:T(8,128)(2,1)}) %all-gather.6.cloned.1.call-update) | async-done | bytes 13762576 | tf_op jit(solution)/shard_map/all_gather | solution.py:121
  140.8 20.3 %pick.2 = (bf16[4,192,4480]{2,1,0:T(8,128)(2,1)}, bf16[4,192,4480]{2,1,0:T(8,128)(2,1)}) custom-call(bf16[4,192,8960]{2,1,0:T(8,128)(2,1)} %all-gather.6.cloned.1.call-done.w_ref), custom_call_target="tpu_custom_call" | custom-call | tf_op jit(solution)/shard_map/pick/pallas_call | solution.py:72
  161.1 6.6 fusion.39
  167.7 0.5 collective-permute-start
  168.2 5.8 pick.3
  174.0 9.8 collective-permute-done.6.other_ref
  183.8 1.3 copy-done.8
  185.0 5.4 join.1
  190.7 18.0 %merge.2 = bf16[4,2,192,4480]{3,2,1,0:T(8,128)(2,1)} custom-call(bf16[4,192,4480]{2,1,0:T(8,128)(2,1)} %get-tuple-element.14.keep_ref, bf16[4,192,4480]{2,1,0:T(8,128)(2,1)} %collective-permute-done.1.take_ref), custom_call_target="tpu_custom_call" | custom-call | tf_op jit(solution)/shard_map/merge/pallas_call | solution.py:118
  208.7 80.9 %fusion.13 = (bf16[4096,4480]{1,0:T(8,128)(2,1)}, bf16[4096,4480]{1,0:T(8,128)(2,1)}) fusion(bf16[1536,4480]{1,0:T(8,128)(2,1)} %bitcast.44, bf16[2048,1536]{1,0:T(8,128)(2,1)} %collective-permute-done, bf16[2048,1536]{1,0:T(8,128)(2,1)} %fusion.39), kind=kOutput, calls=%fused_computation.25 | convolution fusion | flops 56598462464 | bytes 99745792 | tf_op jit(solution)/shard_map/dot_general | solution.py:27
  289.6 18.9 %fusion.56 = f32[1024,1536]{1,0:T(8,128)S(1)} fusion(bf16[4480,1536]{1,0:T(8,128)(2,1)} %bitcast.47, bf16[4096,4480]{1,0:T(8,128)(2,1)} %get-tuple-element.42), kind=kOutput, calls=%fused_computation.81 | convolution fusion | flops 14092861440 | bytes 29229056 | tf_op jit(solution)/shard_map/dot_general | solution.py:27
  308.8 21.8 %fusion.52 = f32[1024,1536]{1,0:T(8,128)} fusion(bf16[4480,1536]{1,0:T(8,128)(2,1)} %bitcast.48, bf16[4096,4480]{1,0:T(8,128)(2,1)} %get-tuple-element.42), kind=kOutput, calls=%fused_computation.77 | convolution fusion | flops 14092861440 | bytes 29229056 | tf_op jit(solution)/shard_map/dot_general | solution.py:27
  330.8 0.3 collective-permute-start.8
  331.1 20.8 %fusion.62 = (f32[1024]{0:T(1024)S(1)}, bf16[1024,1536]{1,0:T(8,128)(2,1)S(1)}) fusion(f32[1024,1536]{1,0:T(8,128)S(1)} %collective-permute-done.2, bf16[4480,1536]{1,0:T(8,128)(2,1)} %bitcast.49, bf16[4096,4480]{1,0:T(8,128)(2,1)} %get-tuple-element.42, bf16[2048,1536]{1,0:T(8,128)(2,1)S(1)} %bitcast.39), kind=kOutput, calls=%fused_computation.92 | convolution fusion | flops 14103870464 | bytes 35524608 | tf_op jit(solution)/shard_map/dot_general | solution.py:27
  351.9 0.6 fusion.63
  352.8 22.7 %fusion.64 = (f32[1024]{0:T(1024)S(1)}, bf16[1024,1536]{1,0:T(8,128)(2,1)S(1)}) fusion(f32[1024,1536]{1,0:T(8,128)} %collective-permute-done.3, bf16[4480,1536]{1,0:T(8,128)(2,1)} %bitcast.50, bf16[4096,4480]{1,0:T(8,128)(2,1)} %get-tuple-element.42, bf16[2048,1536]{1,0:T(8,128)(2,1)S(1)} %bitcast.39), kind=kOutput, calls=%fused_computation.94 | convolution fusion | flops 14103870464 | bytes 35524608 | tf_op jit(solution)/shard_map/dot_general | solution.py:27
  375.5 1.6 copy-done.5
  377.1 2.2 fusion.65
  379.6 5.9 constant_dynamic-update-slice_fusion.1
  385.5 5.9 constant_dynamic-update-slice_fusion
  391.4 6.8 all-gather.12.cloned.1.call-done
  398.3 86.9 %fusion.19 = (bf16[4096,4480]{1,0:T(8,128)(2,1)}, bf16[4096,4480]{1,0:T(8,128)(2,1)}) fusion(bf16[1536,4480]{1,0:T(8,128)(2,1)} %bitcast.55, bf16[1024,1536]{1,0:T(8,128)(2,1)} %collective-permute-done.5, bf16[1024,1536]{1,0:T(8,128)(2,1)} %collective-permute-done.4, bf16[1024,1536]{1,0:T(8,128)(2,1)} %fusion.65, bf16[1024,1536]{1,0:T(8,128)(2,1)S(1)} %fusion.63), kind=kOutput, calls=%fused_computation.31 | convolution fusion | flops 56623628288 | bytes 99745792 | tf_op jit(solution)/shard_map/dot_general | solution.py:27
  485.2 41.9 %all-gather.10.cloned.1.call-done = bf16[4,1120,1536]{2,1,0:T(8,128)(2,1)} async-done(((bf16[1,1120,1536]{2,1,0:T(8,128)(2,1)}), bf16[4,1120,1536]{2,1,0:T(8,128)(2,1)}) %all-gather.10.cloned.1.call-update) | async-done | bytes 13762576 | tf_op jit(solution)/shard_map/all_gather | solution.py:121
  527.1 115.1 %fusion.4 = bf16[4096,4480]{1,0:T(8,128)(2,1)} fusion(bf16[4096,4480]{1,0:T(8,128)(2,1)} %get-tuple-element.49, bf16[4096,1536]{1,0:T(8,128)(2,1)} %constant_dynamic-update-slice_fusion, bf16[4480,1536]{1,0:T(8,128)(2,1)} %bitcast.52), kind=kOutput, calls=%fused_computation.16 | convolution fusion | flops 56793497600 | bytes 99745792 | tf_op jit(solution)/shard_map/dot_general | solution.py:27
  642.2 81.3 %fusion.70 = f32[1536,4480]{1,0:T(8,128)} fusion(bf16[4096,4480]{1,0:T(8,128)(2,1)} %fusion.4, bf16[1024,1536]{1,0:T(8,128)(2,1)} %collective-permute-done.5, bf16[1024,1536]{1,0:T(8,128)(2,1)} %collective-permute-done.4, bf16[1024,1536]{1,0:T(8,128)(2,1)} %fusion.65, bf16[1024,1536]{1,0:T(8,128)(2,1)S(1)} %copy-done.7), kind=kOutput, calls=%fused_computation.103 | convolution fusion | flops 56421777408 | bytes 76808192 | tf_op jit(solution)/shard_map/dot_general | solution.py:27
  723.7 39.1 %fusion.26 = f32[2048,1536]{1,0:T(8,128)} fusion(bf16[1536,4480]{1,0:T(8,128)(2,1)} %bitcast.56, bf16[4096,4480]{1,0:T(8,128)(2,1)} %fusion.4), kind=kOutput, calls=%fused_computation.52 | convolution fusion | flops 28185722880 | bytes 44695552 | tf_op jit(solution)/shard_map/dot_general | solution.py:27
  762.8 68.5 %fusion.84 = f32[4480,1536]{1,0:T(8,128)} fusion(bf16[4096,4480]{1,0:T(8,128)(2,1)} %get-tuple-element.48, bf16[4096,1536]{1,0:T(8,128)(2,1)} %constant_dynamic-update-slice_fusion), kind=kOutput, calls=%fused_computation.129 | convolution fusion | flops 56371445760 | bytes 76808192 | tf_op jit(solution)/shard_map/dot_general | solution.py:27
  831.3 1.9 copy-done.3
  833.2 39.6 %fusion.42 = (f32[2048]{0:T(1024)S(1)}, f32[2048]{0:T(1024)S(1)}, f32[2048,1536]{1,0:T(8,128)}) fusion(bf16[1024,1536]{1,0:T(8,128)(2,1)} %copy-done.5, bf16[1024,1536]{1,0:T(8,128)(2,1)S(1)} %copy-done.3, f32[2048,1536]{1,0:T(8,128)} %collective-permute-done.9, bf16[1536,4480]{1,0:T(8,128)(2,1)} %bitcast.57, bf16[4096,4480]{1,0:T(8,128)(2,1)} %fusion.4), kind=kOutput, calls=%fused_computation.70 | convolution fusion | flops 28214030336 | bytes 63586304 | tf_op jit(solution)/shard_map/dot_general | solution.py:27
  872.8 10.1 fusion.35
  882.9 2.7 copy-done.1
  885.6 0.3 collective-permute-start.10
  885.9 9.9 collective-permute-done.10
  895.8 2.7 copy-done.13
  898.5 110.6 %fusion.7 = bf16[4096,4480]{1,0:T(8,128)(2,1)} fusion(bf16[4096,4480]{1,0:T(8,128)(2,1)} %get-tuple-element.43, bf16[4480,1536]{1,0:T(8,128)(2,1)} %bitcast.51, bf16[2048,1536]{1,0:T(8,128)(2,1)} %copy-done.13, bf16[2048,1536]{1,0:T(8,128)(2,1)} %copy-done.1), kind=kOutput, calls=%fused_computation.19 | convolution fusion | flops 56818663424 | bytes 99745792 | tf_op jit(solution)/shard_map/dot_general | solution.py:27
  1009.1 71.7 %fusion.61 = f32[1536,4480]{1,0:T(8,128)} fusion(bf16[4096,4480]{1,0:T(8,128)(2,1)} %fusion.7, bf16[2048,1536]{1,0:T(8,128)(2,1)} %collective-permute-done, bf16[2048,1536]{1,0:T(8,128)(2,1)} %fusion.39), kind=kOutput, calls=%fused_computation.86 | convolution fusion | flops 56396611584 | bytes 76808192 | tf_op jit(solution)/shard_map/dot_general | solution.py:27
  1080.9 68.2 %fusion.60 = f32[4480,1536]{1,0:T(8,128)} fusion(bf16[4096,4480]{1,0:T(8,128)(2,1)} %get-tuple-element.42, bf16[2048,1536]{1,0:T(8,128)(2,1)} %copy-done.13, bf16[2048,1536]{1,0:T(8,128)(2,1)} %copy-done.1), kind=kOutput, calls=%fused_computation.85 | convolution fusion | flops 56396611584 | bytes 76808192 | tf_op jit(solution)/shard_map/dot_general | solution.py:27
  1149.4 38.6 %fusion.30 = f32[2048,1536]{1,0:T(8,128)} fusion(bf16[4480,1536]{1,0:T(8,128)(2,1)} %bitcast.53, bf16[4096,4480]{1,0:T(8,128)(2,1)} %get-tuple-element.48), kind=kOutput, calls=%fused_computation.56 | convolution fusion | flops 28185722880 | bytes 44695552 | tf_op jit(solution)/shard_map/dot_general | solution.py:27
  1188.0 0.5 collective-permute-start.7
  1188.5 17.8 %merge.3 = bf16[4,2,192,4480]{3,2,1,0:T(8,128)(2,1)} custom-call(bf16[4,192,4480]{2,1,0:T(8,128)(2,1)} %get-tuple-element.14.keep_ref, bf16[4,192,4480]{2,1,0:T(8,128)(2,1)} %collective-permute-done.11.take_ref), custom_call_target="tpu_custom_call" | custom-call | tf_op jit(solution)/shard_map/merge/pallas_call | solution.py:118
  1206.3 38.0 %fusion.22 = f32[2048,1536]{1,0:T(8,128)} fusion(bf16[1536,4480]{1,0:T(8,128)(2,1)} %bitcast.42, bf16[4096,4480]{1,0:T(8,128)(2,1)} %fusion.7), kind=kOutput, calls=%fused_computation.48 | convolution fusion | flops 28185722880 | bytes 44695552 | tf_op jit(solution)/shard_map/dot_general | solution.py:27
  1244.3 0.4 collective-permute-start.12
  1244.7 39.7 %fusion.41 = bf16[2048,1536]{1,0:T(8,128)(2,1)} fusion(f32[2048,1536]{1,0:T(8,128)} %collective-permute-done.7, bf16[4480,1536]{1,0:T(8,128)(2,1)} %bitcast.54, bf16[4096,4480]{1,0:T(8,128)(2,1)} %get-tuple-element.48, bf16[1024,1536]{1,0:T(8,128)(2,1)} %copy-done.5, bf16[1024,1536]{1,0:T(8,128)(2,1)S(1)} %copy-done.4), kind=kOutput, calls=%fused_computation.69 | convolution fusion | flops 28207742976 | bytes 57278464 | tf_op jit(solution)/shard_map/dot_general | solution.py:27
  1284.4 40.1 %fusion.40 = (f32[2048]{0:T(1024)S(1)}, f32[2048,1536]{1,0:T(8,128)}) fusion(bf16[2048,1536]{1,0:T(8,128)(2,1)} %param.4, f32[2048,1536]{1,0:T(8,128)} %collective-permute-done.12, bf16[1536,4480]{1,0:T(8,128)(2,1)} %bitcast.43, bf16[4096,4480]{1,0:T(8,128)(2,1)} %fusion.7), kind=kOutput, calls=%fused_computation.68 | convolution fusion | flops 28198303744 | bytes 63578112 | tf_op jit(solution)/shard_map/dot_general | solution.py:27
  1324.6 5.3 slice_select_fusion
  1329.9 0.4 collective-permute-start.14
  1330.3 0.8 copy-done
  1331.0 11.7 fusion.37
  1342.8 11.6 pad_maximum_fusion.1
  1354.4 81.2 %reduce-scatter.5.cloned.1.call-done = f32[384,4480]{1,0:T(8,128)} async-done(((f32[1536,4480]{1,0:T(8,128)}), f32[384,4480]{1,0:T(8,128)}) %reduce-scatter.5.cloned.1.call-update) | async-done | bytes 6881296 | tf_op jit(solution)/shard_map/reduce_scatter | solution.py:124
  1435.6 5.1 slice_select_fusion.2
  1440.7 4.8 broadcast_select_fusion
  1445.5 3.2 fusion.82
  1448.7 8.2 concatenate.27
  1456.9 217.0 %reduce-scatter.11.cloned.1.call-done = f32[1120,1536]{1,0:T(8,128)} async-done(((f32[4480,1536]{1,0:T(8,128)}), f32[1120,1536]{1,0:T(8,128)}) %reduce-scatter.11.cloned.1.call-update) | async-done | bytes 6881296 | tf_op jit(solution)/shard_map/reduce_scatter | solution.py:124
  1674.0 6.4 bitcast_dynamic-update-slice_fusion
  1680.3 4.6 broadcast_select_fusion.2
  1684.9 3.2 fusion.80
  1688.1 8.0 concatenate.26
  1696.1 11.0 pad_maximum_fusion
  (72 shorter events, 1.9 us)
Async XLA Ops:
  7.2 133.6 %all-gather.6.cloned.1.call-start = ((), (), s32[]{:S(2)}) async-start(), calls=%async_computation.4 | async-start | bytes 17203200 | tf_op jit(solution)/shard_map/all_gather | solution.py:121
  11.2 278.4 %all-gather.8.cloned.1.call-start = ((), (), s32[]{:S(2)}) async-start(), calls=%async_computation.5 | async-start | bytes 17203200 | tf_op jit(solution)/shard_map/all_gather | solution.py:121
  17.6 380.6 %all-gather.12.cloned.1.call-start = ((), (), s32[]{:S(2)}) async-start(), calls=%async_computation.11 | async-start | bytes 17203200 | tf_op jit(solution)/shard_map/all_gather | solution.py:121
  23.2 0.6 copy-start.9
  23.8 143.9 %copy-start.11 = (f32[2048]{0:T(1024)}, f32[2048]{0:T(1024)S(1)}, u32[]{:S(2)}) copy-start(f32[2048]{0:T(1024)S(1)} %fusion.71) | copy-start | bytes 24580
  161.1 29.6 %collective-permute-start.1 = (bf16[4,192,4480]{2,1,0:T(8,128)(2,1)}, bf16[4,192,4480]{2,1,0:T(8,128)(2,1)}, u32[]{:S(2)}, u32[]{:S(2)}) collective-permute-start(bf16[4,192,4480]{2,1,0:T(8,128)(2,1)} %get-tuple-element.15), channel_id=1, source_target_pairs={{0,1},{1,0},{2,3},{3,2},{4,5},{5,4},{6,7},{7,6}} | collective-permute-start | bytes 20643848 | tf_op jit(solution)/shard_map/ppermute | solution.py:31
  167.7 41.0 %collective-permute-start = (bf16[2048,1536]{1,0:T(8,128)(2,1)}, bf16[2048,1536]{1,0:T(8,128)(2,1)}, u32[]{:S(2)}, u32[]{:S(2)}) collective-permute-start(bf16[2048,1536]{1,0:T(8,128)(2,1)} %fusion.39), channel_id=1, source_target_pairs={{0,1},{1,0},{2,3},{3,2},{4,5},{5,4},{6,7},{7,6}} | collective-permute-start | bytes 18874376 | tf_op jit(solution)/shard_map/ppermute | solution.py:31
  174.0 9.8 collective-permute-start.6
  183.8 1.3 copy-start.8
  190.5 336.7 %all-gather.10.cloned.1.call-start = ((), (), s32[]{:S(2)}) async-start(), calls=%async_computation.6 | async-start | bytes 17203200 | tf_op jit(solution)/shard_map/all_gather | solution.py:121
  289.6 41.5 %slice-start = ((s8[6291456]{0:T(1024)(128)(4,1)}), s8[4194304]{0:T(1024)(128)(4,1)S(1)}, s32[]{:S(2)}) async-start(s8[6291456]{0:T(1024)(128)(4,1)} %bitcast.38), calls=%async_computation.12 | async-start | bytes 8388608
  308.5 22.5 %slice-start.1 = ((s8[6291456]{0:T(1024)(128)(4,1)}), s8[2097152]{0:T(1024)(128)(4,1)S(1)}, s32[]{:S(2)}) async-start(s8[6291456]{0:T(1024)(128)(4,1)} %bitcast.38), calls=%async_computation.13 | async-start | bytes 4194304
  308.6 22.5 %collective-permute-start.2 = (f32[1024,1536]{1,0:T(8,128)S(1)}, f32[1024,1536]{1,0:T(8,128)S(1)}, u32[]{:S(2)}, u32[]{:S(2)}) collective-permute-start(f32[1024,1536]{1,0:T(8,128)S(1)} %fusion.56), channel_id=1, source_target_pairs={{0,1},{1,0},{2,3},{3,2},{4,5},{5,4},{6,7},{7,6}} | collective-permute-start | bytes 18874376 | tf_op jit(solution)/shard_map/ppermute | solution.py:31
  330.6 22.2 %collective-permute-start.3 = (f32[1024,1536]{1,0:T(8,128)}, f32[1024,1536]{1,0:T(8,128)}, u32[]{:S(2)}, u32[]{:S(2)}) collective-permute-start(f32[1024,1536]{1,0:T(8,128)} %fusion.52), channel_id=1, source_target_pairs={{0,1},{1,0},{2,3},{3,2},{4,5},{5,4},{6,7},{7,6}} | collective-permute-start | bytes 18874376 | tf_op jit(solution)/shard_map/ppermute | solution.py:31
  330.8 54.7 %collective-permute-start.8 = (bf16[2048,1536]{1,0:T(8,128)(2,1)}, bf16[2048,1536]{1,0:T(8,128)(2,1)}, u32[]{:S(2)}, u32[]{:S(2)}) collective-permute-start(bf16[2048,1536]{1,0:T(8,128)(2,1)} %param.5), channel_id=1, source_target_pairs={{0,1},{1,0},{2,3},{3,2},{4,5},{5,4},{6,7},{7,6}} | collective-permute-start | bytes 18874376 | tf_op jit(solution)/shard_map/ppermute | solution.py:31
  351.9 23.6 %copy-start.2 = (bf16[1024,1536]{1,0:T(8,128)(2,1)}, bf16[1024,1536]{1,0:T(8,128)(2,1)S(1)}, u32[]{:S(2)}) copy-start(bf16[1024,1536]{1,0:T(8,128)(2,1)S(1)} %get-tuple-element.47) | copy-start | bytes 9437188
  352.5 45.8 %copy-start.6 = (bf16[1024,1536]{1,0:T(8,128)(2,1)}, bf16[1024,1536]{1,0:T(8,128)(2,1)S(1)}, u32[]{:S(2)}) copy-start(bf16[1024,1536]{1,0:T(8,128)(2,1)S(1)} %fusion.63) | copy-start | bytes 9437188
  352.5 45.8 %collective-permute-start.4 = (bf16[1024,1536]{1,0:T(8,128)(2,1)S(1)}, bf16[1024,1536]{1,0:T(8,128)(2,1)}, u32[]{:S(2)}, u32[]{:S(2)}) collective-permute-start(bf16[1024,1536]{1,0:T(8,128)(2,1)S(1)} %fusion.63), channel_id=1, source_target_pairs={{0,1},{1,0},{2,3},{3,2},{4,5},{5,4},{6,7},{7,6}} | collective-permute-start | bytes 9437192 | tf_op jit(solution)/shard_map/ppermute | solution.py:31
  375.5 1.6 copy-start.5
  379.3 18.9 %collective-permute-start.5 = (bf16[1024,1536]{1,0:T(8,128)(2,1)}, bf16[1024,1536]{1,0:T(8,128)(2,1)}, u32[]{:S(2)}, u32[]{:S(2)}) collective-permute-start(bf16[1024,1536]{1,0:T(8,128)(2,1)} %fusion.65), channel_id=1, source_target_pairs={{0,1},{1,0},{2,3},{3,2},{4,5},{5,4},{6,7},{7,6}} | collective-permute-start | bytes 9437192 | tf_op jit(solution)/shard_map/ppermute | solution.py:31
  379.6 945.0 %reduce-scatter.7.cloned.1.call-start = ((), (), s32[]{:S(2)}) async-start(), calls=%async_computation.8 | async-start | bytes 34406400 | tf_op jit(solution)/shard_map/reduce_scatter | solution.py:124
  527.1 115.1 %copy-start.7 = (bf16[1024,1536]{1,0:T(8,128)(2,1)S(1)}, bf16[1024,1536]{1,0:T(8,128)(2,1)}, u32[]{:S(2)}) copy-start(bf16[1024,1536]{1,0:T(8,128)(2,1)} %copy-done.6) | copy-start | bytes 9437188
  723.6 619.2 %reduce-scatter.9.cloned.1.call-start = ((), (), s32[]{:S(2)}) async-start(), calls=%async_computation.9 | async-start | bytes 34406400 | tf_op jit(solution)/shard_map/reduce_scatter | solution.py:124
  762.8 68.5 %collective-permute-start.9 = (f32[2048,1536]{1,0:T(8,128)}, f32[2048,1536]{1,0:T(8,128)}, u32[]{:S(2)}, u32[]{:S(2)}) collective-permute-start(f32[2048,1536]{1,0:T(8,128)} %fusion.26), channel_id=1, source_target_pairs={{0,1},{1,0},{2,3},{3,2},{4,5},{5,4},{6,7},{7,6}} | collective-permute-start | bytes 37748744 | tf_op jit(solution)/shard_map/ppermute | solution.py:31
  831.2 2.0 copy-start.3
  831.2 604.3 %reduce-scatter.5.cloned.1.call-start = ((), (), s32[]{:S(2)}) async-start(), calls=%async_computation.7 | async-start | bytes 34406400 | tf_op jit(solution)/shard_map/reduce_scatter | solution.py:124
  882.9 2.7 copy-start.1
  885.6 10.2 collective-permute-start.10
  895.8 2.7 copy-start.13
  1080.8 593.1 %reduce-scatter.11.cloned.1.call-start = ((), (), s32[]{:S(2)}) async-start(), calls=%async_computation.10 | async-start | bytes 34406400 | tf_op jit(solution)/shard_map/reduce_scatter | solution.py:124
  1149.1 39.3 %collective-permute-start.11 = (bf16[4,192,4480]{2,1,0:T(8,128)(2,1)}, bf16[4,192,4480]{2,1,0:T(8,128)(2,1)}, u32[]{:S(2)}, u32[]{:S(2)}) collective-permute-start(bf16[4,192,4480]{2,1,0:T(8,128)(2,1)} %get-tuple-element.15), channel_id=1, source_target_pairs={{0,1},{1,0},{2,3},{3,2},{4,5},{5,4},{6,7},{7,6}} | collective-permute-start | bytes 20643848 | tf_op jit(solution)/shard_map/ppermute | solution.py:31
  1188.0 56.7 %collective-permute-start.7 = (f32[2048,1536]{1,0:T(8,128)}, f32[2048,1536]{1,0:T(8,128)}, u32[]{:S(2)}, u32[]{:S(2)}) collective-permute-start(f32[2048,1536]{1,0:T(8,128)} %fusion.30), channel_id=1, source_target_pairs={{0,1},{1,0},{2,3},{3,2},{4,5},{5,4},{6,7},{7,6}} | collective-permute-start | bytes 37748744 | tf_op jit(solution)/shard_map/ppermute | solution.py:31
  1206.3 38.5 %copy-start.4 = (bf16[1024,1536]{1,0:T(8,128)(2,1)S(1)}, bf16[1024,1536]{1,0:T(8,128)(2,1)}, u32[]{:S(2)}) copy-start(bf16[1024,1536]{1,0:T(8,128)(2,1)} %copy-done.2) | copy-start | bytes 9437188
  1244.3 40.1 %collective-permute-start.12 = (f32[2048,1536]{1,0:T(8,128)}, f32[2048,1536]{1,0:T(8,128)}, u32[]{:S(2)}, u32[]{:S(2)}) collective-permute-start(f32[2048,1536]{1,0:T(8,128)} %fusion.22), channel_id=1, source_target_pairs={{0,1},{1,0},{2,3},{3,2},{4,5},{5,4},{6,7},{7,6}} | collective-permute-start | bytes 37748744 | tf_op jit(solution)/shard_map/ppermute | solution.py:31
  1284.4 40.2 %copy-start.10 = (f32[2048]{0:T(1024)S(1)}, f32[2048]{0:T(1024)}, u32[]{:S(2)}) copy-start(f32[2048]{0:T(1024)} %copy-done.9) | copy-start | bytes 24580
  1284.4 45.9 %copy-start.12 = (f32[2048]{0:T(1024)S(1)}, f32[2048]{0:T(1024)}, u32[]{:S(2)}) copy-start(f32[2048]{0:T(1024)} %copy-done.11) | copy-start | bytes 24580
  1324.6 6.5 copy-start
  1329.9 110.9 %collective-permute-start.14 = (f32[192,4480]{1,0:T(8,128)}, f32[192,4480]{1,0:T(8,128)S(1)}, u32[]{:S(2)}, u32[]{:S(2)}) collective-permute-start(f32[192,4480]{1,0:T(8,128)} %slice_select_fusion), channel_id=1, source_target_pairs={{0,1},{1,0},{2,3},{3,2},{4,5},{5,4},{6,7},{7,6}} | collective-permute-start | bytes 10321928 | tf_op jit(solution)/shard_map/ppermute | solution.py:31
  1440.7 239.6 %collective-permute-start.13 = (f32[192,4480]{1,0:T(8,128)}, f32[192,4480]{1,0:T(8,128)}, u32[]{:S(2)}, u32[]{:S(2)}) collective-permute-start(f32[192,4480]{1,0:T(8,128)} %slice_select_fusion.2), channel_id=1, source_target_pairs={{0,1},{1,0},{2,3},{3,2},{4,5},{5,4},{6,7},{7,6}} | collective-permute-start | bytes 10321928 | tf_op jit(solution)/shard_map/ppermute | solution.py:31
Sparse Core Ops, SparseCore 0:
  11.3 129.4 all-gather.5
  143.1 126.6 all-gather.7
  271.6 126.6 all-gather.11
  400.5 126.6 all-gather.9
  723.7 235.2 reduce-scatter.6
  961.9 235.2 reduce-scatter.8
  1200.3 235.2 reduce-scatter.4
  1438.6 235.2 reduce-scatter.10
